TPU v7x, 32 devices: a whole 2x2x4 slice. The times are simulated.
32 devices in a mesh: col: 8 (over y, x, core), grp: 4 (over z).
Axes of the slice: x: 2, y: 2, z: 4, core: 2. Of those that a mesh axis runs over, the one named last changes fastest.
Arguments:
- profiles: float32 [2048, 116], P('col'), may hold values from -6 to 6
- courant: float32 [2048, 58], P('col'), may hold values from -0.7 to 0.7
- owner_map: int32 [2048], replicated, may hold values from 0 to 2047, as said below
- cloud_flags: int32 [2048], P('col'), may hold values 0 or 1
- crm_state: float32 [2, 58, 64, 2048], P(None, None, 'grp', 'col'), may hold values from -6 to 6
Outputs:
- tendency: float32 [2048, 116], P('col')
- crm_final: float32 [2, 58, 64, 2048], P(None, None, 'grp', 'col')
Inputs may be any that keep to these rules, and one draw needn't show every extreme that they name: owner_map is a permutation; physics column p lives in span p // 256, element column e in group e // 256; each group hands at most 34 columns to one span, and exactly 34 to some spans, and every span receives exactly 256 columns.
All inputs are finite; a program needn't handle non-finite values. No bound on the sum of `cloud_flags` on one device may be relied on, other than what follows from the above.
Results may differ from a plain program's by a relative error of at most 0.00002.
Values sent between devices are 32-bit elements; how exact they have to be, the bound alone decides.
A program may use at most 64 MiB of HBM per device.

v0:
```python
import functools

import jax
import jax.numpy as jnp
from jax import lax
from jax.experimental import pallas as pl
from jax.experimental.pallas import tpu as pltpu
from jax.sharding import PartitionSpec as P

STEPS = 8
DEPTH = 4
LANES = 128
LIMIT = 36 * 2**20
TOP = 8
MESH = pl.DeviceIdType.MESH
HIGHEST = lax.Precision.HIGHEST

diffuse_x = 0.25
diffuse_z = 0.2
sat_scale = 0.5
sat_slope = 0.3
cond_rate = 0.5
latent_gain = 0.4
LOG2E = 1.4426950408889634


def round_up(n, m):
    return -(-n // m) * m


def contract(a, b, dims):
    return lax.dot_general(
        a, b, (dims, ((), ())), precision=HIGHEST, preferred_element_type=jnp.float32
    )


def window_kernel(
    depth,
    prof_ref,
    cour_ref,
    owner_ref,
    cloud_ref,
    x_ref,
    land,
    give,
    final_ref,
    xs,
    outs,
    buf,
    sends,
    gets,
    take,
    fsend,
    fland,
    force,
    wind,
    part,
    heap,
    mine,
    inc,
    pack,
    local_sem,
    halo_sem,
    force_sem,
    sum_sem,
    back_sem,
):
    fields, levels, cells = xs.shape[1:4]
    chunks = xs.shape[0]
    groups, cap = fland.shape[:2]
    columns = chunks * LANES
    peers = lax.axis_size("grp")
    z_me = lax.axis_index("grp")
    c_me = lax.axis_index("col")
    rounds = STEPS // depth
    width = cells + 2 * depth
    span = lambda i: pl.ds(i * LANES, LANES)

    loads = []
    for c in range(chunks):
        load = pltpu.make_async_copy(
            x_ref.at[:, :, :, span(c)], xs.at[c], local_sem.at[0, c]
        )
        load.start()
        loads.append(load)

    barrier = pltpu.get_barrier_semaphore()
    for k in range(1, peers):
        pl.semaphore_signal(
            barrier, inc=1, device_id={"grp": lax.rem(z_me + k, peers)}, device_id_type=MESH
        )
    for k in range(1, groups):
        pl.semaphore_signal(
            barrier, inc=1, device_id={"col": lax.rem(c_me + k, groups)}, device_id_type=MESH
        )

    def halo_copies(c, r):
        copies = []
        for side in range(2):
            peer = lax.rem(z_me + (peers - 1 if side == 0 else 1), peers)
            copies.append(
                pltpu.make_async_remote_copy(
                    src_ref=sends.at[c, r, side],
                    dst_ref=gets.at[c, r, side],
                    send_sem=halo_sem.at[0, c, r, side],
                    recv_sem=halo_sem.at[1, c, r, side],
                    device_id={"grp": peer},
                    device_id_type=MESH,
                )
            )
        return copies

    waits = []
    for c in range(chunks):
        loads[c].wait()

        def fill(z, carry):
            for f in range(fields):
                x = xs[c, f, z]
                buf[c, 0, f, z, TOP : TOP + cells] = x
                sends[c, 0, 0, f, z] = x[:depth]
                sends[c, 0, 1, f, z] = x[cells - depth :]
            return carry

        lax.fori_loop(0, levels, fill, 0)
        if c == 0:
            pl.semaphore_wait(barrier, peers - 1 + groups - 1)
        for copy in halo_copies(c, 0):
            copy.start()
            waits.append(copy)

    owner = jnp.concatenate(
        [owner_ref[pl.ds(c, groups, stride=chunks), :] for c in range(chunks)], axis=1
    )
    own_row = jnp.concatenate(
        [owner_ref[pl.ds(c_me * chunks + c, 1), :] for c in range(chunks)], axis=1
    )
    group_ids = lax.broadcasted_iota(jnp.int32, (groups, columns), 0)
    earlier = (
        lax.broadcasted_iota(jnp.int32, (columns, columns), 0)
        < lax.broadcasted_iota(jnp.int32, (columns, columns), 1)
    ).astype(jnp.float32)
    slot = lax.broadcasted_iota(jnp.int32, (cap, columns), 0).astype(jnp.float32)
    spot = lax.broadcasted_iota(jnp.int32, (cap, columns), 1).astype(jnp.float32) + 1.0

    def ranked(hits):
        rank = jnp.dot(hits, earlier, preferred_element_type=jnp.float32)
        return jnp.where(hits > 0.5, rank, -1.0)

    low = own_row - group_ids * columns
    order = ranked(jnp.where((low >= 0) & (low < columns), 1.0, 0.0))
    for q in range(groups):
        give[q * cap : (q + 1) * cap, :] = jnp.where(order[q : q + 1] == slot, 1.0, 0.0)

    for f, ref in ((0, prof_ref), (1, cour_ref)):
        lines = ref.shape[0]
        fsend[:, :, f * LANES : f * LANES + lines] = contract(
            give[...], ref[...], ((1,), (1,))
        ).reshape(groups, cap, lines)
    shares = []
    for k in range(1, groups):
        peer = lax.rem(c_me + k, groups)
        copy = pltpu.make_async_remote_copy(
            src_ref=fsend.at[peer],
            dst_ref=fland.at[c_me],
            send_sem=force_sem.at[0, k],
            recv_sem=force_sem.at[1, k],
            device_id={"col": peer},
            device_id_type=MESH,
        )
        copy.start()
        shares.append(copy)
    waits += shares
    fland[c_me] = fsend[c_me]

    local = owner - c_me * columns
    order = ranked(jnp.where((local >= 0) & (local < columns), 1.0, 0.0))
    place = (local + 1).astype(jnp.float32)
    for q in range(groups):
        chosen = jnp.where(order[q : q + 1] == slot, place[q : q + 1], 0.0)
        chosen = jnp.sum(chosen, axis=1, keepdims=True)
        take[q * cap : (q + 1) * cap, :] = jnp.where(chosen == spot, 1.0, 0.0)

    for copy in shares:
        copy.wait_recv()
    phys = contract(
        fland[:, :, :LANES].reshape(groups * cap, LANES), take[...], ((0,), (0,))
    )
    for f in range(fields):
        for c in range(chunks):
            force[c, f] = (
                phys[f * levels : (f + 1) * levels, c * LANES : (c + 1) * LANES] / STEPS
            )
    phys = contract(
        fland[:, :, LANES:].reshape(groups * cap, LANES), take[...], ((0,), (0,))
    )
    for c in range(chunks):
        wind[c] = phys[:levels, c * LANES : (c + 1) * LANES]
    half_cloud = cond_rate * cloud_ref[...].astype(jnp.float32)

    def stepped(c, src, z, count):
        up = jnp.minimum(z + 1, levels - 1)
        down = jnp.maximum(z - 1, 0)
        lanes = slice(c * LANES, (c + 1) * LANES)
        speed = 0.5 * wind[c, pl.ds(z, 1), :]
        new = []
        for f in range(fields):
            here = buf[c, src, f, z, TOP : TOP + count]
            west = buf[c, src, f, z, TOP - 1 : TOP - 1 + count]
            east = buf[c, src, f, z, TOP + 1 : TOP + 1 + count]
            upper = buf[c, src, f, up, TOP : TOP + count]
            lower = buf[c, src, f, down, TOP : TOP + count]
            new.append(
                (1.0 - 2.0 * diffuse_x - 2.0 * diffuse_z) * here
                + ((diffuse_x + speed) * west + (diffuse_x - speed) * east)
                + (diffuse_z * (upper + lower) + force[c, f, pl.ds(z, 1), :])
            )
        energy, moisture = new
        excess = (moisture + sat_scale) - sat_scale * jnp.exp2((sat_slope * LOG2E) * energy)
        amount = jnp.maximum(excess, 0.0) * half_cloud[:, lanes]
        return energy + latent_gain * amount, moisture - amount

    def sweep(c, src):
        def level(z, carry):
            for f, value in enumerate(stepped(c, src, z, width)):
                buf[c, 1 - src, f, z, TOP : TOP + width] = value
                buf[c, 1 - src, f, z, TOP - 1 : TOP] = value[width - 1 :]
                buf[c, 1 - src, f, z, TOP + width : TOP + width + 1] = value[:1]
            return carry

        lax.fori_loop(0, levels, level, 0, unroll=2)

    def last(c, src):
        def level(z, carry):
            for f, value in enumerate(stepped(c, src, z, cells)):
                outs[c, f, z] = value
                part[c, pl.ds(f * levels + z, 1), :] = jnp.sum(
                    value - xs[c, f, z], axis=0, keepdims=True
                )
            return carry

        lax.fori_loop(0, levels, level, 0, unroll=2)

    lines = part.shape[1] // peers
    block = lambda i: pl.ds(pl.multiple_of(i * lines, lines), lines)

    def sum_copies(c, phase):
        copies = []
        for k in range(1, peers):
            peer = lax.rem(z_me + k, peers)
            if phase == 0:
                source, target = part.at[c, block(peer)], heap.at[c, k]
            else:
                source, target = mine.at[c], inc.at[c, block(z_me)]
            copies.append(
                pltpu.make_async_remote_copy(
                    src_ref=source,
                    dst_ref=target,
                    send_sem=sum_sem.at[phase, 0, c, k],
                    recv_sem=sum_sem.at[phase, 1, c, k],
                    device_id={"grp": peer},
                    device_id_type=MESH,
                )
            )
        for copy in copies:
            copy.start()
            waits.append(copy)
        return copies

    def add_up(c, scatter):
        total = part[c, block(z_me), :]
        for k, copy in enumerate(scatter):
            copy.wait_recv()
            total = total + heap[c, k + 1]
        total = total / (cells * peers)
        mine[c] = total
        inc[c, block(z_me), :] = total
        return sum_copies(c, 1)

    pad_rows = part.shape[1] - fields * levels
    if pad_rows:
        for c in range(chunks):
            part[c, fields * levels :, :] = jnp.zeros((pad_rows, LANES), jnp.float32)

    scatters, gathers, stores = [], [], []
    for r in range(rounds):
        for c in range(chunks):
            for copy in halo_copies(c, r):
                copy.wait_recv()
            src = (r * depth) % 2

            def widen(z, carry):
                for f in range(fields):
                    right = gets[c, r, 0, f, z]
                    left = gets[c, r, 1, f, z]
                    buf[c, src, f, z, TOP + cells : TOP + cells + depth] = right
                    buf[c, src, f, z, TOP + cells + depth : TOP + width] = left
                    buf[c, src, f, z, TOP - 1 : TOP] = left[depth - 1 :]
                    buf[c, src, f, z, TOP + width : TOP + width + 1] = buf[
                        c, src, f, z, TOP : TOP + 1
                    ]
                return carry

            lax.fori_loop(0, levels, widen, 0)
            final_round = r == rounds - 1
            if final_round and c > 0:
                gathers += add_up(c - 1, scatters[c - 1])
            for s in range(depth - 1 if final_round else depth):
                sweep(c, (src + s) % 2)
            src = (src + depth - (1 if final_round else 0)) % 2
            if not final_round:

                def narrow(z, carry):
                    for f in range(fields):
                        sends[c, r + 1, 0, f, z] = buf[c, src, f, z, TOP : TOP + depth]
                        sends[c, r + 1, 1, f, z] = buf[
                            c, src, f, z, TOP + cells - depth : TOP + cells
                        ]
                    return carry

                lax.fori_loop(0, levels, narrow, 0)
                for copy in halo_copies(c, r + 1):
                    copy.start()
                    waits.append(copy)
            else:
                last(c, src)
                scatters.append(sum_copies(c, 0))
                store = pltpu.make_async_copy(
                    outs.at[c], final_ref.at[:, :, :, span(c)], local_sem.at[1, c]
                )
                store.start()
                stores.append(store)
    gathers += add_up(chunks - 1, scatters[chunks - 1])
    for copy in gathers:
        copy.wait_recv()
    packed = 0.0
    for c in range(chunks):
        packed = packed + contract(
            take[:, c * LANES : (c + 1) * LANES], inc[c], ((1,), (1,))
        )
    pack[...] = packed.reshape(pack.shape)
    returns = []
    for k in range(1, groups):
        peer = lax.rem(c_me + k, groups)
        copy = pltpu.make_async_remote_copy(
            src_ref=pack.at[peer],
            dst_ref=land.at[c_me],
            send_sem=back_sem.at[0, k],
            recv_sem=back_sem.at[1, k],
            device_id={"col": peer},
            device_id_type=MESH,
        )
        copy.start()
        returns.append(copy)
    waits += returns
    land[c_me] = pack[c_me]
    for copy in returns:
        copy.wait_recv()
    for copy in waits:
        copy.wait_send()
    for store in stores:
        store.wait()


def finish_kernel(land_ref, give_ref, state_ref, tend_ref, final_ref, sems):
    fields = state_ref.shape[0]
    store = [
        pltpu.make_async_copy(state_ref.at[f], final_ref.at[f], sems.at[f]) for f in range(fields)
    ]
    for copy in store:
        copy.start()
    groups, cap, rows = land_ref.shape
    back = contract(land_ref[...].reshape(groups * cap, rows), give_ref[...], ((0,), (0,)))
    tend_ref[...] = back[: tend_ref.shape[0]]
    for copy in store:
        copy.wait()


def on_device(profiles, courant, owner_map, cloud_flags, crm_state):
    columns = profiles.shape[0]
    fields, levels, cells = crm_state.shape[:3]
    groups = lax.axis_size("col")
    peers = lax.axis_size("grp")
    per_peer = columns // groups
    cap = round_up(per_peer + min(2, per_peer), 8)
    chunks = columns // LANES
    depth = min(DEPTH, cells)
    rounds = STEPS // depth
    rows = round_up(fields * levels, 8 * peers)
    f32 = lambda *shape: pltpu.VMEM(shape, jnp.float32)
    dma = lambda *shape: pltpu.SemaphoreType.DMA(shape)
    vmem = pl.BlockSpec(memory_space=pltpu.VMEM)
    anywhere = pl.BlockSpec(memory_space=pl.ANY)
    tall = round_up(TOP + cells + 2 * depth + 1, 8)
    land, give, state = pl.pallas_call(
        functools.partial(window_kernel, depth),
        out_shape=(
            jax.ShapeDtypeStruct((groups, cap, rows), jnp.float32),
            jax.ShapeDtypeStruct((groups * cap, columns), jnp.float32),
            jax.ShapeDtypeStruct(crm_state.shape, jnp.float32),
        ),
        in_specs=[vmem, vmem, vmem, vmem, pl.BlockSpec(memory_space=pltpu.HBM)],
        out_specs=(vmem, vmem, anywhere),
        scratch_shapes=[
            f32(chunks, fields, levels, cells, LANES),
            f32(chunks, fields, levels, cells, LANES),
            f32(chunks, 2, fields, levels, tall, LANES),
            f32(chunks, rounds, 2, fields, levels, depth, LANES),
            f32(chunks, rounds, 2, fields, levels, depth, LANES),
            f32(groups * cap, columns),
            f32(groups, cap, 2 * LANES),
            f32(groups, cap, 2 * LANES),
            f32(chunks, fields, levels, LANES),
            f32(chunks, levels, LANES),
            f32(chunks, rows, LANES),
            f32(chunks, peers, rows // peers, LANES),
            f32(chunks, rows // peers, LANES),
            f32(chunks, rows, LANES),
            f32(groups, cap, rows),
            dma(2, chunks),
            dma(2, chunks, rounds, 2),
            dma(2, groups),
            dma(2, 2, chunks, peers),
            dma(2, groups),
        ],
        compiler_params=pltpu.CompilerParams(
            collective_id=0, has_side_effects=True, vmem_limit_bytes=LIMIT
        ),
    )(
        profiles.T,
        courant.T,
        owner_map.reshape(groups * chunks, LANES),
        cloud_flags[None, :],
        crm_state,
    )
    tendency, final = pl.pallas_call(
        finish_kernel,
        out_shape=(
            jax.ShapeDtypeStruct((fields * levels, columns), jnp.float32),
            jax.ShapeDtypeStruct(crm_state.shape, jnp.float32),
        ),
        in_specs=[vmem, vmem, anywhere],
        out_specs=(vmem, anywhere),
        scratch_shapes=[dma(fields)],
        compiler_params=pltpu.CompilerParams(vmem_limit_bytes=4 * 2**20),
    )(land, give, state)
    return tendency.T, final


def solution(mesh):
    placed = (P("col", None), P("col", None), P(), P("col"), P(None, None, "grp", "col"))
    return jax.shard_map(
        on_device,
        mesh=mesh,
        in_specs=placed,
        out_specs=(P("col", None), P(None, None, "grp", "col")),
        check_vma=False,
    )
```

profile of v0, /device:TPU:0, one launch (start us, length us, event | category | flops | bytes accessed | tf_op | source)
XLA Modules:
  0.0 75.1 jit_solution(7285671973907305929)
XLA Ops:
  0.6 0.0 copy-start
  0.6 1.5 %copy-done = f32[2,58,16,256]{3,2,1,0:T(8,128)S(1)} copy-done((f32[2,58,16,256]{3,2,1,0:T(8,128)S(1)}, f32[2,58,16,256]{3,2,1,0:T(8,128)}, u32[]{:S(2)}) %copy-start) | copy-done | bytes 1900568
  2.2 0.0 copy-start.1
  2.2 0.9 %copy-done.1 = f32[256,116]{0,1:T(8,128)S(1)} copy-done((f32[256,116]{0,1:T(8,128)S(1)}, f32[256,116]{0,1:T(8,128)}, u32[]{:S(2)}) %copy-start.1) | copy-done | bytes 118808
  3.1 0.0 copy-start.2
  3.1 0.8 %copy-done.2 = f32[256,58]{0,1:T(8,128)S(1)} copy-done((f32[256,58]{0,1:T(8,128)S(1)}, f32[256,58]{0,1:T(8,128)}, u32[]{:S(2)}) %copy-start.2) | copy-done | bytes 59416
  3.9 0.0 copy-start.3
  3.9 0.7 copy-done.3
  4.6 0.0 copy-start.4
  4.6 0.7 copy-done.4
  5.3 67.9 %shard_map.68 = (f32[8,40,128]{2,1,0:T(8,128)S(1)}, f32[320,256]{1,0:T(8,128)S(1)}, f32[2,58,16,256]{3,2,1,0:T(8,128)S(1)}) custom-call(f32[116,256]{1,0:T(8,128)S(1)} %bitcast.5, f32[58,256]{1,0:T(8,128)S(1)} %bitcast.6, s32[16,128]{1,0:T(8,128)S(1)} %bitcast.7, s32[1,256]{1,0:T(1,128)S(1)} %bitcast.8, f32[2,58,16,256]{3,2,1,0:T(8,128)S(1)} %copy-done), custom_call_target="tpu_custom_call" | custom-call | tf_op jit(solution)/shard_map/pallas_call | solution.py:395
  73.2 1.9 %shard_map.69 = (f32[116,256]{1,0:T(8,128)}, f32[2,58,16,256]{3,2,1,0:T(8,128)}) custom-call(f32[8,40,128]{2,1,0:T(8,128)S(1)} %get-tuple-element.7.land_ref, f32[320,256]{1,0:T(8,128)S(1)} %get-tuple-element.8.give_ref, f32[2,58,16,256]{3,2,1,0:T(8,128)S(1)} %get-tuple-element.9.state_ref), custom_call_target="tpu_custom_call" | custom-call | tf_op jit(solution)/shard_map/pallas_call | solution.py:436
Async XLA Ops:
  0.6 1.5 %copy-start = (f32[2,58,16,256]{3,2,1,0:T(8,128)S(1)}, f32[2,58,16,256]{3,2,1,0:T(8,128)}, u32[]{:S(2)}) copy-start(f32[2,58,16,256]{3,2,1,0:T(8,128)} %x_ref.1) | copy-start | bytes 5701636
  2.2 0.9 %copy-start.1 = (f32[256,116]{0,1:T(8,128)S(1)}, f32[256,116]{0,1:T(8,128)}, u32[]{:S(2)}) copy-start(f32[256,116]{0,1:T(8,128)} %param.5) | copy-start | bytes 356356
  3.1 0.8 %copy-start.2 = (f32[256,58]{0,1:T(8,128)S(1)}, f32[256,58]{0,1:T(8,128)}, u32[]{:S(2)}) copy-start(f32[256,58]{0,1:T(8,128)} %param.6) | copy-start | bytes 178180
  3.9 0.7 copy-start.3
  4.6 0.7 copy-start.4
where the time goes:
time: 75.4 us; the launch traced here: 75.1 us
  Pallas kernels  69.9 us (93%)
  local copies, waits for them, and re-layouts  4.63 us (6%)
    pallas_call x1, Pallas kernels, on_device(): pl.pallas_call(functools.partial(window_kernel, depth), out_shape=(jax.Sh...  67.9 us
    unnamed x10, local copies, waits for them, and re-layouts  4.63 us
    pallas_call x1, Pallas kernels, on_device(): pl.pallas_call(finish_kernel, out_shape=(jax.ShapeDtypeStruct((fields * l...  1.93 us

commit v1 on v0

v1 whole, which is shorter than its diff:
```python
import functools

import jax
import jax.numpy as jnp
from jax import lax
from jax.experimental import pallas as pl
from jax.experimental.pallas import tpu as pltpu
from jax.sharding import PartitionSpec as P

STEPS = 8
DEPTH = STEPS
BLOCK = 8
LANES = 128
LIMIT = int(50 * 2**20)
TOP = 8
MESH = pl.DeviceIdType.MESH
HIGHEST = lax.Precision.HIGHEST

diffuse_x = 0.25
diffuse_z = 0.2
sat_scale = 0.5
sat_slope = 0.3
cond_rate = 0.5
latent_gain = 0.4
LOG2E = 1.4426950408889634


def round_up(n, m):
    return -(-n // m) * m


def contract(a, b, dims):
    return lax.dot_general(
        a, b, (dims, ((), ())), precision=HIGHEST, preferred_element_type=jnp.float32
    )


def window_kernel(
    prof_hbm,
    cour_hbm,
    owner_hbm,
    cloud_hbm,
    x_hbm,
    land,
    give,
    final_ref,
    prof_ref,
    cour_ref,
    owner_ref,
    cloud_ref,
    wide,
    slabs,
    odd,
    even,
    take,
    fsend,
    fland,
    force,
    wind,
    part,
    heap,
    mine,
    inc,
    pack,
    local_sem,
    halo_sem,
    force_sem,
    sum_sem,
    back_sem,
):
    fields, levels, cells, columns = x_hbm.shape
    chunks = columns // LANES
    groups, cap = fland.shape[:2]
    peers = lax.axis_size("grp")
    z_me = lax.axis_index("grp")
    c_me = lax.axis_index("col")
    direct = cells % 8 == 0
    reach = 1 if direct else DEPTH // cells
    width = cells + 2 * DEPTH
    own = TOP + DEPTH
    blocks = -(-levels // BLOCK)
    middle = blocks - 2
    tail = levels - (blocks - 1) * BLOCK
    span = lambda i: pl.ds(i * LANES, LANES)

    loads = []
    for c in range(chunks):
        if direct:
            target = wide.at[c, :, :, own : own + cells, :]
        else:
            target = slabs.at[c, 2 * reach]
        load = pltpu.make_async_copy(x_hbm.at[:, :, :, span(c)], target, local_sem.at[c])
        load.start()
        loads.append(load)
    small = []
    pairs = ((prof_hbm, prof_ref), (cour_hbm, cour_ref), (owner_hbm, owner_ref), (cloud_hbm, cloud_ref))
    for i, (source, target) in enumerate(pairs):
        load = pltpu.make_async_copy(source, target, local_sem.at[chunks + i])
        load.start()
        small.append(load)

    barrier = pltpu.get_barrier_semaphore()
    for k in range(1, peers):
        pl.semaphore_signal(
            barrier, inc=1, device_id={"grp": lax.rem(z_me + k, peers)}, device_id_type=MESH
        )
    for k in range(1, groups):
        pl.semaphore_signal(
            barrier, inc=1, device_id={"col": lax.rem(c_me + k, groups)}, device_id_type=MESH
        )

    def halo_copies(c, b, count):
        rows = pl.ds(b * BLOCK, count)
        copies = []
        for j in range(1, reach + 1):
            for side in range(2):
                peer = lax.rem(z_me + (peers - j if side == 0 else j), peers)
                slot = 2 * (j - 1) + side
                if direct:
                    near = own if side == 0 else own + cells - DEPTH
                    far = own + cells if side == 0 else TOP
                    source = wide.at[c, :, rows, near : near + DEPTH, :]
                    target = wide.at[c, :, rows, far : far + DEPTH, :]
                else:
                    source = slabs.at[c, 2 * reach, :, rows]
                    target = slabs.at[c, slot, :, rows]
                copies.append(
                    pltpu.make_async_remote_copy(
                        src_ref=source,
                        dst_ref=target,
                        send_sem=halo_sem.at[0, c, b, slot],
                        recv_sem=halo_sem.at[1, c, b, slot],
                        device_id={"grp": peer},
                        device_id_type=MESH,
                    )
                )
        return copies

    size = lambda b: BLOCK if b < blocks - 1 else tail
    waits = []
    with jax.named_scope("barrier"):
        pl.semaphore_wait(barrier, peers - 1 + groups - 1)
    with jax.named_scope("send"):
        for c in range(chunks):
            loads[c].wait()
            for b in range(blocks):
                for copy in halo_copies(c, b, size(b)):
                    copy.start()
                    waits.append(copy)

    with jax.named_scope("forcing"):
        for load in small:
            load.wait()
        owner = jnp.concatenate(
            [owner_ref[pl.ds(c, groups, stride=chunks), :] for c in range(chunks)], axis=1
        )
        own_row = jnp.concatenate(
            [owner_ref[pl.ds(c_me * chunks + c, 1), :] for c in range(chunks)], axis=1
        )
        group_ids = lax.broadcasted_iota(jnp.int32, (groups, columns), 0)
        earlier = (
            lax.broadcasted_iota(jnp.int32, (columns, columns), 0)
            < lax.broadcasted_iota(jnp.int32, (columns, columns), 1)
        ).astype(jnp.float32)
        slot = lax.broadcasted_iota(jnp.int32, (cap, columns), 0).astype(jnp.float32)
        spot = lax.broadcasted_iota(jnp.int32, (cap, columns), 1).astype(jnp.float32) + 1.0

        def ranked(hits):
            rank = jnp.dot(hits, earlier, preferred_element_type=jnp.float32)
            return jnp.where(hits > 0.5, rank, -1.0)

        low = own_row - group_ids * columns
        order = ranked(jnp.where((low >= 0) & (low < columns), 1.0, 0.0))
        for q in range(groups):
            give[q * cap : (q + 1) * cap, :] = jnp.where(order[q : q + 1] == slot, 1.0, 0.0)

        for f, ref in ((0, prof_ref), (1, cour_ref)):
            lines = ref.shape[0]
            fsend[:, :, f * LANES : f * LANES + lines] = contract(
                give[...], ref[...], ((1,), (1,))
            ).reshape(groups, cap, lines)
        shares = []
        for k in range(1, groups):
            peer = lax.rem(c_me + k, groups)
            copy = pltpu.make_async_remote_copy(
                src_ref=fsend.at[peer],
                dst_ref=fland.at[c_me],
                send_sem=force_sem.at[0, k],
                recv_sem=force_sem.at[1, k],
                device_id={"col": peer},
                device_id_type=MESH,
            )
            copy.start()
            shares.append(copy)
        waits += shares
        fland[c_me] = fsend[c_me]

        local = owner - c_me * columns
        order = ranked(jnp.where((local >= 0) & (local < columns), 1.0, 0.0))
        place = (local + 1).astype(jnp.float32)
        for q in range(groups):
            chosen = jnp.where(order[q : q + 1] == slot, place[q : q + 1], 0.0)
            chosen = jnp.sum(chosen, axis=1, keepdims=True)
            take[q * cap : (q + 1) * cap, :] = jnp.where(chosen == spot, 1.0, 0.0)

    with jax.named_scope("force_wait"):
        for copy in shares:
            copy.wait_recv()
    with jax.named_scope("force_take"):
        phys = contract(
            fland[:, :, :LANES].reshape(groups * cap, LANES), take[...], ((0,), (0,))
        )
        for f in range(fields):
            for c in range(chunks):
                force[c, f] = (
                    phys[f * levels : (f + 1) * levels, c * LANES : (c + 1) * LANES] / STEPS
                )
        phys = contract(
            fland[:, :, LANES:].reshape(groups * cap, LANES), take[...], ((0,), (0,))
        )
        for c in range(chunks):
            wind[c] = phys[:levels, c * LANES : (c + 1) * LANES]
    half_cloud = cond_rate * cloud_ref[...].astype(jnp.float32)

    def stepped(c, s, z):
        rows = width - 2 * s if s == STEPS else round_up(width - 2 * s, 8)
        first = TOP + (width - rows) // 2
        source = wide.at[c] if s == 1 else (odd if s % 2 == 0 else even)
        up = jnp.minimum(z + 1, levels - 1)
        down = jnp.maximum(z - 1, 0)
        speed = 0.5 * wind[c, pl.ds(z, 1), :]
        new = []
        for f in range(fields):
            here = source[f, z, first : first + rows]
            west = source[f, z, first - 1 : first - 1 + rows]
            east = source[f, z, first + 1 : first + 1 + rows]
            upper = source[f, up, first : first + rows]
            lower = source[f, down, first : first + rows]
            new.append(
                (1.0 - 2.0 * diffuse_x - 2.0 * diffuse_z) * here
                + ((diffuse_x + speed) * west + (diffuse_x - speed) * east)
                + (diffuse_z * (upper + lower) + force[c, f, pl.ds(z, 1), :])
            )
        energy, moisture = new
        excess = (moisture + sat_scale) - sat_scale * jnp.exp2((sat_slope * LOG2E) * energy)
        amount = jnp.maximum(excess, 0.0) * half_cloud[:, c * LANES : (c + 1) * LANES]
        return first, rows, (energy + latent_gain * amount, moisture - amount)

    def put(c, s, z, result):
        first, rows, values = result
        target = odd if s % 2 else even
        for f, value in enumerate(values):
            if s == STEPS:
                final_ref[f, z, :, c * LANES : (c + 1) * LANES] = value
                if direct:
                    old = wide[c, f, z, own : own + cells]
                else:
                    old = slabs[c, 2 * reach, f, z]
                part[c, pl.ds(f * levels + z, 1), :] = jnp.sum(
                    value - old, axis=0, keepdims=True
                )
            else:
                target[f, z, first : first + rows] = value

    def sweep(c, s, low, count):
        def pair(i, carry):
            z = low + 2 * i
            results = [stepped(c, s, z + k) for k in range(2)]
            for k in range(2):
                put(c, s, z + k, results[k])
            return carry

        if count > 1:
            lax.fori_loop(0, count // 2, pair, 0)
        if count % 2:
            z = low + count - 1
            put(c, s, z, stepped(c, s, z))

    def arrive(c, b, count):
        for copy in halo_copies(c, b, count):
            copy.wait_recv()
        if not direct:

            def fill(z, carry):
                for f in range(fields):
                    wide[c, f, z, own : own + cells] = slabs[c, 2 * reach, f, z]
                    for j in range(1, reach + 1):
                        right = own + j * cells
                        left = own - j * cells
                        wide[c, f, z, right : right + cells] = slabs[c, 2 * j - 2, f, z]
                        wide[c, f, z, left : left + cells] = slabs[c, 2 * j - 1, f, z]
                return carry

            lax.fori_loop(b * BLOCK, b * BLOCK + count, fill, 0)

    def wave(c):
        with jax.named_scope(f"first#c={c}"):
            arrive(c, 0, BLOCK)
            for s in range(1, STEPS + 1):
                sweep(c, s, 0, BLOCK - s)

        def body(b, carry):
            with jax.named_scope("arrive"):
                arrive(c, b, BLOCK)
            with jax.named_scope("steps"):
                for s in range(1, STEPS + 1):
                    sweep(c, s, b * BLOCK - s, BLOCK)
            return carry

        lax.fori_loop(1, blocks - 1, body, 0)
        with jax.named_scope("arrive_last"):
            arrive(c, blocks - 1, tail)
        with jax.named_scope("steps_last"):
            for s in range(1, STEPS + 1):
                sweep(c, s, (blocks - 1) * BLOCK - s, tail + s)

    lines = part.shape[1] // peers
    block = lambda i: pl.ds(pl.multiple_of(i * lines, lines), lines)

    def sum_copies(c, phase):
        copies = []
        for k in range(1, peers):
            peer = lax.rem(z_me + k, peers)
            if phase == 0:
                source, target = part.at[c, block(peer)], heap.at[c, k]
            else:
                source, target = mine.at[c], inc.at[c, block(z_me)]
            copies.append(
                pltpu.make_async_remote_copy(
                    src_ref=source,
                    dst_ref=target,
                    send_sem=sum_sem.at[phase, 0, c, k],
                    recv_sem=sum_sem.at[phase, 1, c, k],
                    device_id={"grp": peer},
                    device_id_type=MESH,
                )
            )
        for copy in copies:
            copy.start()
            waits.append(copy)
        return copies

    def add_up(c, scatter):
        total = part[c, block(z_me), :]
        for k, copy in enumerate(scatter):
            copy.wait_recv()
            total = total + heap[c, k + 1]
        total = total / (cells * peers)
        mine[c] = total
        inc[c, block(z_me), :] = total
        return sum_copies(c, 1)

    pad_rows = part.shape[1] - fields * levels
    if pad_rows:
        for c in range(chunks):
            part[c, fields * levels :, :] = jnp.zeros((pad_rows, LANES), jnp.float32)

    scatters, gathers = [], []
    for c in range(chunks):
        wave(c)
        scatters.append(sum_copies(c, 0))
    with jax.named_scope("add_up"):
        for c in range(chunks):
            gathers += add_up(c, scatters[c])
    with jax.named_scope("gather_wait"):
        for copy in gathers:
            copy.wait_recv()
    with jax.named_scope("pack"):
        packed = 0.0
        for c in range(chunks):
            packed = packed + contract(
                take[:, c * LANES : (c + 1) * LANES], inc[c], ((1,), (1,))
            )
        pack[...] = packed.reshape(pack.shape)
    returns = []
    for k in range(1, groups):
        peer = lax.rem(c_me + k, groups)
        copy = pltpu.make_async_remote_copy(
            src_ref=pack.at[peer],
            dst_ref=land.at[c_me],
            send_sem=back_sem.at[0, k],
            recv_sem=back_sem.at[1, k],
            device_id={"col": peer},
            device_id_type=MESH,
        )
        copy.start()
        returns.append(copy)
    waits += returns
    land[c_me] = pack[c_me]
    with jax.named_scope("return_wait"):
        for copy in returns:
            copy.wait_recv()
    with jax.named_scope("drain"):
        for copy in waits:
            copy.wait_send()


def finish_kernel(land_ref, give_ref, state_ref, tend_ref, final_ref, sems):
    fields = state_ref.shape[0]
    store = [
        pltpu.make_async_copy(state_ref.at[f], final_ref.at[f], sems.at[f]) for f in range(fields)
    ]
    for copy in store:
        copy.start()
    groups, cap, rows = land_ref.shape
    back = contract(land_ref[...].reshape(groups * cap, rows), give_ref[...], ((0,), (0,)))
    tend_ref[...] = back[: tend_ref.shape[0]]
    for copy in store:
        copy.wait()


def on_device(profiles, courant, owner_map, cloud_flags, crm_state):
    columns = profiles.shape[0]
    fields, levels, cells = crm_state.shape[:3]
    groups = lax.axis_size("col")
    peers = lax.axis_size("grp")
    per_peer = columns // groups
    cap = round_up(per_peer + min(2, per_peer), 8)
    chunks = columns // LANES
    direct = cells % 8 == 0
    reach = 1 if direct else DEPTH // cells
    blocks = -(-levels // BLOCK)
    rows = round_up(fields * levels, 8 * peers)
    f32 = lambda *shape: pltpu.VMEM(shape, jnp.float32)
    i32 = lambda *shape: pltpu.VMEM(shape, jnp.int32)
    dma = lambda *shape: pltpu.SemaphoreType.DMA(shape)
    vmem = pl.BlockSpec(memory_space=pltpu.VMEM)
    anywhere = pl.BlockSpec(memory_space=pl.ANY)
    tall = round_up(TOP + cells + 2 * DEPTH + 1, 8)
    slabs = (8, 128) if direct else (chunks, 2 * reach + 1, fields, levels, cells, LANES)
    land, give, state = pl.pallas_call(
        window_kernel,
        out_shape=(
            jax.ShapeDtypeStruct((groups, cap, rows), jnp.float32),
            jax.ShapeDtypeStruct((groups * cap, columns), jnp.float32),
            jax.ShapeDtypeStruct(crm_state.shape, jnp.float32),
        ),
        in_specs=[anywhere] * 5,
        out_specs=(vmem, vmem, vmem),
        scratch_shapes=[
            f32(fields * levels, columns),
            f32(levels, columns),
            i32(groups * chunks, LANES),
            i32(1, columns),
            f32(chunks, fields, levels, tall, LANES),
            f32(*slabs),
            f32(fields, levels, tall, LANES),
            f32(fields, levels, tall, LANES),
            f32(groups * cap, columns),
            f32(groups, cap, 2 * LANES),
            f32(groups, cap, 2 * LANES),
            f32(chunks, fields, levels, LANES),
            f32(chunks, levels, LANES),
            f32(chunks, rows, LANES),
            f32(chunks, peers, rows // peers, LANES),
            f32(chunks, rows // peers, LANES),
            f32(chunks, rows, LANES),
            f32(groups, cap, rows),
            dma(chunks + 4),
            dma(2, chunks, blocks, 2 * reach),
            dma(2, groups),
            dma(2, 2, chunks, peers),
            dma(2, groups),
        ],
        compiler_params=pltpu.CompilerParams(
            collective_id=0, has_side_effects=True, vmem_limit_bytes=LIMIT
        ),
    )(
        profiles.T,
        courant.T,
        owner_map.reshape(groups * chunks, LANES),
        cloud_flags[None, :],
        crm_state,
    )
    tendency, final = pl.pallas_call(
        finish_kernel,
        out_shape=(
            jax.ShapeDtypeStruct((fields * levels, columns), jnp.float32),
            jax.ShapeDtypeStruct(crm_state.shape, jnp.float32),
        ),
        in_specs=[vmem, vmem, anywhere],
        out_specs=(vmem, anywhere),
        scratch_shapes=[dma(fields)],
        compiler_params=pltpu.CompilerParams(vmem_limit_bytes=4 * 2**20),
    )(land, give, state)
    return tendency.T, final


def solution(mesh):
    placed = (P("col", None), P("col", None), P(), P("col"), P(None, None, "grp", "col"))
    return jax.shard_map(
        on_device,
        mesh=mesh,
        in_specs=placed,
        out_specs=(P("col", None), P(None, None, "grp", "col")),
        check_vma=False,
    )
```

time: 75.4 us -> 70.3 us (0.932)
  Pallas kernels: 69.9 us -> 66.3 us
  local copies, waits for them, and re-layouts: 4.63 us -> 3.11 us
    pallas_call x1, Pallas kernels: 67.9 us -> 64.4 us  [on_device(): pl.pallas_call(window_kernel, out_shape=(jax.ShapeDtypeStruct((groups, ca...]
    unnamed x10 -> x8, local copies, waits for them, and re-layouts: 4.63 us -> 3.11 us
where the time goes in v1:
time: 70.3 us; the launch traced here: 70.1 us
  Pallas kernels  66.3 us (94%)
  local copies, waits for them, and re-layouts  3.11 us (4%)
    pallas_call x1, Pallas kernels, on_device(): pl.pallas_call(window_kernel, out_shape=(jax.ShapeDtypeStruct((groups, ca...  64.4 us
    unnamed x8, local copies, waits for them, and re-layouts  3.11 us
    pallas_call x1, Pallas kernels, on_device(): pl.pallas_call(finish_kernel, out_shape=(jax.ShapeDtypeStruct((fields * l...  1.93 us

profile of v1, /device:TPU:0, one launch (start us, length us, event | category | flops | bytes accessed | tf_op | source)
XLA Modules:
  0.0 70.1 jit_solution(5722856701206234269)
XLA Ops:
  0.6 0.0 copy-start
  0.6 0.9 %copy-done = f32[256,116]{0,1:T(8,128)S(1)} copy-done((f32[256,116]{0,1:T(8,128)S(1)}, f32[256,116]{0,1:T(8,128)}, u32[]{:S(2)}) %copy-start) | copy-done | bytes 118808
  1.5 0.0 copy-start.1
  1.5 0.8 %copy-done.1 = f32[256,58]{0,1:T(8,128)S(1)} copy-done((f32[256,58]{0,1:T(8,128)S(1)}, f32[256,58]{0,1:T(8,128)}, u32[]{:S(2)}) %copy-start.1) | copy-done | bytes 59416
  2.4 0.0 copy-start.2
  2.4 0.7 copy-done.2
  3.1 0.0 copy-start.3
  3.1 0.7 copy-done.3
  3.8 64.4 %shard_map.68 = (f32[8,40,128]{2,1,0:T(8,128)S(1)}, f32[320,256]{1,0:T(8,128)S(1)}, f32[2,58,16,256]{3,2,1,0:T(8,128)S(1)}) custom-call(f32[116,256]{1,0:T(8,128)S(1)} %bitcast.5, f32[58,256]{1,0:T(8,128)S(1)} %bitcast.6, s32[16,128]{1,0:T(8,128)S(1)} %bitcast.7, s32[1,256]{1,0:T(1,128)S(1)} %bitcast.8, f32[2,58,16,256]{3,2,1,0:T(8,128)} %x_hbm.1), custom_call_target="tpu_custom_call" | custom-call | tf_op jit(solution)/shard_map/pallas_call | solution.py:431
  68.1 1.9 %shard_map.69 = (f32[116,256]{1,0:T(8,128)}, f32[2,58,16,256]{3,2,1,0:T(8,128)}) custom-call(f32[8,40,128]{2,1,0:T(8,128)S(1)} %get-tuple-element.7.land_ref, f32[320,256]{1,0:T(8,128)S(1)} %get-tuple-element.8.give_ref, f32[2,58,16,256]{3,2,1,0:T(8,128)S(1)} %get-tuple-element.9.state_ref), custom_call_target="tpu_custom_call" | custom-call | tf_op jit(solution)/shard_map/pallas_call | solution.py:475
Async XLA Ops:
  0.6 0.9 %copy-start = (f32[256,116]{0,1:T(8,128)S(1)}, f32[256,116]{0,1:T(8,128)}, u32[]{:S(2)}) copy-start(f32[256,116]{0,1:T(8,128)} %param.5) | copy-start | bytes 356356
  1.5 0.8 %copy-start.1 = (f32[256,58]{0,1:T(8,128)S(1)}, f32[256,58]{0,1:T(8,128)}, u32[]{:S(2)}) copy-start(f32[256,58]{0,1:T(8,128)} %param.6) | copy-start | bytes 178180
  2.4 0.7 copy-start.2
  3.1 0.7 copy-start.3

commit v2 on v1

v2 whole, which is shorter than its diff:
```python
import jax
import jax.numpy as jnp
from jax import lax
from jax.experimental import pallas as pl
from jax.experimental.pallas import tpu as pltpu
from jax.sharding import PartitionSpec as P

STEPS = 8
DEPTH = STEPS
BLOCK = 8
PIECE = 4
LANES = 128
LIMIT = 67_043_328
TOP = 8
MESH = pl.DeviceIdType.MESH

diffuse_x = 0.25
diffuse_z = 0.2
sat_scale = 0.5
sat_slope = 0.3
cond_rate = 0.5
latent_gain = 0.4
SCALE = sat_slope * 1.4426950408889634


def round_up(n, m):
    return -(-n // m) * m


def parts_of(x):
    high = x.astype(jnp.bfloat16)
    rest = x - high.astype(jnp.float32)
    middle = rest.astype(jnp.bfloat16)
    return high, middle, (rest - middle.astype(jnp.float32)).astype(jnp.bfloat16)


def pick(parts, hot, dims, swap=False):
    total = 0.0
    for part in parts:
        pair = (hot, part) if swap else (part, hot)
        total = total + lax.dot_general(
            *pair, (dims, ((), ())), preferred_element_type=jnp.float32
        )
    return total


def level_edges(levels):
    full = max(2, (levels - BLOCK) // BLOCK)
    edges = [i * BLOCK for i in range(full + 1)]
    while edges[-1] < levels:
        edges.append(min(edges[-1] + PIECE, levels))
    return full, edges


def window_kernel(
    prof_hbm,
    cour_hbm,
    owner_hbm,
    cloud_hbm,
    x_hbm,
    land,
    give_hbm,
    final_hbm,
    prof_ref,
    cour_ref,
    owner_ref,
    cloud_ref,
    wide,
    slabs,
    odd,
    even,
    outs,
    give,
    take,
    fsend,
    fland,
    coef,
    whole,
    early,
    late,
    heap,
    early_heap,
    late_heap,
    mine,
    early_mine,
    inc,
    early_inc,
    pack,
    load_sem,
    out_sem,
    halo_send,
    halo_recv,
    swap_sem,
    sum_sem,
):
    fields, levels, cells, columns = x_hbm.shape
    chunks = columns // LANES
    groups, cap = fland.shape[:2]
    peers = lax.axis_size("grp")
    z_me = lax.axis_index("grp")
    c_me = lax.axis_index("col")
    direct = cells % 8 == 0
    reach = 1 if direct else DEPTH // cells
    width = cells + 2 * DEPTH
    own = TOP + DEPTH
    full, edges = level_edges(levels)
    split = (full - 1) * BLOCK
    span = lambda i: pl.ds(i * LANES, LANES)

    loads = []
    for c in range(chunks):
        if direct:
            target = wide.at[c, :, :, own : own + cells, :]
        else:
            target = slabs.at[c, 2 * reach]
        load = pltpu.make_async_copy(x_hbm.at[:, :, :, span(c)], target, load_sem.at[c])
        load.start()
        loads.append(load)
    small = []
    pairs = ((prof_hbm, prof_ref), (cour_hbm, cour_ref), (owner_hbm, owner_ref), (cloud_hbm, cloud_ref))
    for i, (source, target) in enumerate(pairs):
        load = pltpu.make_async_copy(source, target, load_sem.at[chunks + i])
        load.start()
        small.append(load)

    barrier = pltpu.get_barrier_semaphore()
    for k in range(1, peers):
        pl.semaphore_signal(
            barrier, inc=1, device_id={"grp": lax.rem(z_me + k, peers)}, device_id_type=MESH
        )
    for k in range(1, groups):
        pl.semaphore_signal(
            barrier, inc=1, device_id={"col": lax.rem(c_me + k, groups)}, device_id_type=MESH
        )

    def remote(source, target, send, recv, axis, peer):
        return pltpu.make_async_remote_copy(
            src_ref=source,
            dst_ref=target,
            send_sem=send,
            recv_sem=recv,
            device_id={axis: peer},
            device_id_type=MESH,
        )

    def received(ref, sem):
        remote(ref, ref, sem, sem, "grp", z_me).wait_recv()

    def sent(ref, sem):
        remote(ref, ref, sem, sem, "grp", z_me).wait_send()

    def send_halos(c, b):
        rows = pl.ds(edges[b], edges[b + 1] - edges[b])
        for j in range(1, reach + 1):
            for side in range(2):
                peer = lax.rem(z_me + (peers - j if side == 0 else j), peers)
                if direct:
                    near = own if side == 0 else own + cells - DEPTH
                    far = own + cells if side == 0 else TOP
                    source = wide.at[c, :, rows, near : near + DEPTH, :]
                    target = wide.at[c, :, rows, far : far + DEPTH, :]
                else:
                    source = slabs.at[c, 2 * reach, :, rows]
                    target = slabs.at[c, 2 * (j - 1) + side, :, rows]
                remote(source, target, halo_send.at[0], halo_recv.at[c, b], "grp", peer).start()

    with jax.named_scope("barrier"):
        pl.semaphore_wait(barrier, peers - 1 + groups - 1)
    with jax.named_scope("send"):
        for c in range(chunks):
            loads[c].wait()
            for b in range(len(edges) - 1):
                send_halos(c, b)

    with jax.named_scope("forcing"):
        for load in small:
            load.wait()
        owner = jnp.concatenate(
            [owner_ref[pl.ds(c, groups, stride=chunks), :] for c in range(chunks)], axis=1
        )
        own_row = jnp.concatenate(
            [owner_ref[pl.ds(c_me * chunks + c, 1), :] for c in range(chunks)], axis=1
        )
        group_ids = lax.broadcasted_iota(jnp.int32, (groups, columns), 0)
        earlier = (
            lax.broadcasted_iota(jnp.int32, (columns, columns), 0)
            < lax.broadcasted_iota(jnp.int32, (columns, columns), 1)
        ).astype(jnp.float32)
        slot = lax.broadcasted_iota(jnp.int32, (cap, columns), 0).astype(jnp.float32)
        spot = lax.broadcasted_iota(jnp.int32, (cap, columns), 1).astype(jnp.float32) + 1.0

        def ranked(hits):
            rank = jnp.dot(hits, earlier, preferred_element_type=jnp.float32)
            return jnp.where(hits > 0.5, rank, -1.0)

        low = own_row - group_ids * columns
        order = ranked(jnp.where((low >= 0) & (low < columns), 1.0, 0.0))
        for q in range(groups):
            hot = jnp.where(order[q : q + 1] == slot, 1.0, 0.0)
            give[q * cap : (q + 1) * cap, :] = hot
        give_out = pltpu.make_async_copy(give, give_hbm, out_sem.at[0])
        give_out.start()

        for f, ref in ((0, prof_ref), (1, cour_ref)):
            lines = ref.shape[0]
            fsend[:, :, f * LANES : f * LANES + lines] = pick(
                parts_of(ref[...]), give[...].astype(jnp.bfloat16), ((1,), (1,)), swap=True
            ).reshape(groups, cap, lines)
        for k in range(1, groups):
            peer = lax.rem(c_me + k, groups)
            remote(
                fsend.at[peer], fland.at[c_me], swap_sem.at[0], swap_sem.at[1], "col", peer
            ).start()
        fland[c_me] = fsend[c_me]

        local = owner - c_me * columns
        order = ranked(jnp.where((local >= 0) & (local < columns), 1.0, 0.0))
        place = (local + 1).astype(jnp.float32)
        for q in range(groups):
            chosen = jnp.where(order[q : q + 1] == slot, place[q : q + 1], 0.0)
            chosen = jnp.sum(chosen, axis=1, keepdims=True)
            take[q * cap : (q + 1) * cap, :] = jnp.where(chosen == spot, 1.0, 0.0)
        hot = take[...].astype(jnp.bfloat16)

    with jax.named_scope("force_wait"):
        received(fland.at[pl.ds(0, groups - 1)], swap_sem.at[1])
    with jax.named_scope("force_take"):
        landed = fland[:, :, :LANES].reshape(groups * cap, LANES)
        phys = pick(parts_of(landed), hot, ((0,), (0,))) / STEPS
        landed = fland[:, :, LANES:].reshape(groups * cap, LANES)
        speed = 0.5 * pick(parts_of(landed), hot, ((0,), (0,)))
        for c in range(chunks):
            lanes = slice(c * LANES, (c + 1) * LANES)
            west = diffuse_x + speed[:levels, lanes]
            east = diffuse_x - speed[:levels, lanes]
            heat = SCALE * phys[:levels, lanes]
            rain = phys[levels : 2 * levels, lanes]
            rows = (SCALE * west, west, SCALE * east, east, heat - 1.0, rain + sat_scale, heat, rain)
            for i, row in enumerate(rows):
                coef[c, i] = row
    rain_gain = cond_rate * cloud_ref[...].astype(jnp.float32)
    heat_gain = (latent_gain * SCALE) * rain_gain

    def stepped(c, s, z):
        rows = width - 2 * s if s == STEPS else round_up(width - 2 * s, 8)
        first = TOP + (width - rows) // 2
        source = wide.at[c] if s == 1 else (odd if s % 2 == 0 else even)
        if isinstance(z, int):
            up, down = min(z + 1, levels - 1), max(z - 1, 0)
        else:
            up, down = jnp.minimum(z + 1, levels - 1), jnp.maximum(z - 1, 0)
        lanes = slice(c * LANES, (c + 1) * LANES)
        new = []
        for f in range(fields):
            scale = SCALE if s == 1 and f == 0 else 1.0
            pick_row = lambda i: coef[c, i, pl.ds(z, 1), :]
            west_gain = pick_row(0 if scale != 1.0 else 1)
            east_gain = pick_row(2 if scale != 1.0 else 3)
            push = pick_row((4 if s == 1 else 6) + f)
            here = source[f, z, first : first + rows]
            west = source[f, z, first - 1 : first - 1 + rows]
            east = source[f, z, first + 1 : first + 1 + rows]
            upper = source[f, up, first : first + rows]
            lower = source[f, down, first : first + rows]
            new.append(
                (
                    (scale * (1.0 - 2.0 * diffuse_x - 2.0 * diffuse_z)) * here
                    + (scale * diffuse_z) * (upper + lower)
                )
                + ((west_gain * west + east_gain * east) + push)
            )
        energy, moisture = new
        excess = jnp.maximum(moisture - jnp.exp2(energy), 0.0)
        energy = energy + excess * heat_gain[:, lanes]
        moisture = moisture - excess * rain_gain[:, lanes]
        if s == STEPS:
            energy = energy * (1.0 / SCALE) + 1.0 / SCALE
            moisture = moisture - sat_scale
        return first, rows, (energy, moisture)

    def put(c, s, z, result, sums, row):
        first, rows, values = result
        target = odd if s % 2 else even
        for f, value in enumerate(values):
            if s == STEPS:
                outs[f, z, :, c * LANES : (c + 1) * LANES] = value
                if direct:
                    old = wide[c, f, z, own : own + cells]
                else:
                    old = slabs[c, 2 * reach, f, z]
                sums[pl.ds(row(f, z), 1), :] = jnp.sum(value - old, axis=0, keepdims=True)
            else:
                target[f, z, first : first + rows] = value

    def sweep(c, s, low, count, sums, row, unroll):
        def body(i, carry):
            z = low + unroll * i
            results = [stepped(c, s, z + k) for k in range(unroll)]
            for k in range(unroll):
                put(c, s, z + k, results[k], sums, row)
            return carry

        trips = count // unroll
        if trips == 1:
            body(0, 0)
        elif trips > 1:
            lax.fori_loop(0, trips, body, 0)
        rest = [low + k for k in range(trips * unroll, count)]
        results = [stepped(c, s, z) for z in rest]
        for z, result in zip(rest, results):
            put(c, s, z, result, sums, row)

    def arrive(c, b, start, count):
        rows = pl.ds(start, count)
        if direct:
            received(wide.at[c, :, rows, TOP : TOP + 2 * DEPTH, :], halo_recv.at[c, b])
        else:
            received(slabs.at[c, pl.ds(0, 2 * reach), :, rows], halo_recv.at[c, b])

            def fill(z, carry):
                for f in range(fields):
                    wide[c, f, z, own : own + cells] = slabs[c, 2 * reach, f, z]
                    for j in range(1, reach + 1):
                        right = own + j * cells
                        left = own - j * cells
                        wide[c, f, z, right : right + cells] = slabs[c, 2 * j - 2, f, z]
                        wide[c, f, z, left : left + cells] = slabs[c, 2 * j - 1, f, z]
                return carry

            lax.fori_loop(start, start + count, fill, 0)

    def opening(c, sums, row):
        with jax.named_scope(f"first#c={c}"):
            arrive(c, 0, 0, BLOCK)
            for s in range(1, STEPS + 1):
                sweep(c, s, 0, BLOCK - s, sums, row, 2)

        def body(b, carry):
            with jax.named_scope("arrive"):
                arrive(c, b, b * BLOCK, BLOCK)
            with jax.named_scope("steps"):
                for s in range(1, STEPS + 1):
                    sweep(c, s, b * BLOCK - s, BLOCK, sums, row, 4)
            return carry

        lax.fori_loop(1, full, body, 0)

    def scatter(part, landing, sem):
        lines = part.shape[0] // peers
        for k in range(1, peers):
            peer = lax.rem(z_me + k, peers)
            block = pl.ds(pl.multiple_of(peer * lines, lines), lines)
            remote(part.at[block], landing.at[k - 1], sem.at[0], sem.at[1], "grp", peer).start()

    def gather(part, landing, piece, result, sem, sem2):
        lines = part.shape[0] // peers
        block = pl.ds(pl.multiple_of(z_me * lines, lines), lines)
        total = part[block, :]
        received(landing, sem.at[1])
        for k in range(peers - 1):
            total = total + landing[k]
        piece[...] = total
        result[block, :] = total
        for k in range(1, peers):
            peer = lax.rem(z_me + k, peers)
            remote(piece, result.at[block], sem2.at[0], sem2.at[1], "grp", peer).start()

    def others(ref):
        return ref.at[pl.ds(0, ref.shape[0] // peers * (peers - 1))]

    last = chunks - 1
    for c in range(last):
        whole[c, fields * levels :, :] = jnp.zeros_like(whole[c, fields * levels :, :])
        row = lambda f, z: f * levels + z
        opening(c, whole.at[c], row)
        for b in range(full, len(edges) - 1):
            arrive(c, b, edges[b], edges[b + 1] - edges[b])
        with jax.named_scope("closing"):
            for s in range(1, STEPS + 1):
                sweep(c, s, edges[full] - s, levels - edges[full] + s, whole.at[c], row, 2)
        scatter(whole.at[c], heap.at[c], sum_sem.at[2 * c])
        pltpu.make_async_copy(
            outs.at[:, :, :, span(c)], final_hbm.at[:, :, :, span(c)], out_sem.at[1]
        ).start()
    early[fields * split :, :] = jnp.zeros_like(early[fields * split :, :])
    late[fields * (levels - split) :, :] = jnp.zeros_like(late[fields * (levels - split) :, :])
    opening(last, early, lambda f, z: f * split + z)
    scatter(early, early_heap, sum_sem.at[2 * last])
    pltpu.make_async_copy(
        outs.at[:, pl.ds(0, split), :, span(last)],
        final_hbm.at[:, pl.ds(0, split), :, span(last)],
        out_sem.at[1],
    ).start()
    row = lambda f, z: f * (levels - split) + z - split
    for b in range(full, len(edges) - 1):
        with jax.named_scope(f"late_arrive#b={b}"):
            arrive(last, b, edges[b], edges[b + 1] - edges[b])
        with jax.named_scope(f"late_steps#b={b}"):
            ends = b == len(edges) - 2
            for s in range(1, STEPS + 1):
                count = edges[b + 1] - edges[b] + (s if ends else 0)
                sweep(last, s, edges[b] - s, count, late, row, count if ends else 4)
    for k in range(1, peers):
        peer = lax.rem(z_me + k, peers)
        remote(
            late, late_heap.at[k - 1], sum_sem.at[2 * last + 2, 0], sum_sem.at[2 * last + 2, 1], "grp", peer
        ).start()
    pltpu.make_async_copy(
        outs.at[:, pl.ds(split, levels - split), :, span(last)],
        final_hbm.at[:, pl.ds(split, levels - split), :, span(last)],
        out_sem.at[1],
    ).start()
    with jax.named_scope("scatter_wait"):
        for c in range(last):
            gather(whole.at[c], heap.at[c], mine.at[c], inc.at[c], sum_sem.at[2 * c], sum_sem.at[2 * c + 1])
        gather(early, early_heap, early_mine, early_inc, sum_sem.at[2 * last], sum_sem.at[2 * last + 1])
    with jax.named_scope("late_wait"):
        received(late_heap, sum_sem.at[2 * last + 2, 1])
        total = late[...]
        for k in range(peers - 1):
            total = total + late_heap[k]
        for f in range(fields):
            inc[last, f * levels + split : (f + 1) * levels, :] = total[
                f * (levels - split) : (f + 1) * (levels - split)
            ]
        inc[last, fields * levels :, :] = jnp.zeros_like(inc[last, fields * levels :, :])
    with jax.named_scope("gather_wait"):
        packed = 0.0
        for c in range(last):
            received(others(inc.at[c]), sum_sem.at[2 * c + 1, 1])
            packed = packed + pick(
                parts_of(inc[c]), hot[:, c * LANES : (c + 1) * LANES], ((1,), (1,)), swap=True
            )
        received(others(early_inc), sum_sem.at[2 * last + 1, 1])
    with jax.named_scope("pack"):
        for f in range(fields):
            inc[last, f * levels : f * levels + split, :] = early_inc[f * split : (f + 1) * split, :]
        packed = packed + pick(
            parts_of(inc[last]), hot[:, last * LANES :], ((1,), (1,)), swap=True
        )
        pack[...] = (packed / (cells * peers)).reshape(pack.shape)
    for k in range(1, groups):
        peer = lax.rem(c_me + k, groups)
        remote(pack.at[peer], land.at[c_me], swap_sem.at[2], swap_sem.at[3], "col", peer).start()
    keep = pltpu.make_async_copy(pack.at[c_me], land.at[c_me], out_sem.at[2])
    keep.start()
    with jax.named_scope("drain"):
        if direct:
            sent(wide.at[:, :, :, TOP : TOP + 2 * DEPTH, :], halo_send.at[0])
        else:
            sent(slabs.at[:, pl.ds(0, 2 * reach)], halo_send.at[0])
        sent(fsend.at[pl.ds(0, groups - 1)], swap_sem.at[0])
        for c in range(last):
            sent(others(inc.at[c]), sum_sem.at[2 * c, 0])
            sent(others(inc.at[c]), sum_sem.at[2 * c + 1, 0])
        sent(others(early_inc), sum_sem.at[2 * last, 0])
        sent(others(early_inc), sum_sem.at[2 * last + 1, 0])
        sent(late_heap, sum_sem.at[2 * last + 2, 0])
        give_out.wait()
        pltpu.make_async_copy(outs, final_hbm, out_sem.at[1]).wait()
        keep.wait()
        sent(pack.at[pl.ds(0, groups - 1)], swap_sem.at[2])
    with jax.named_scope("return_wait"):
        received(land.at[pl.ds(0, groups - 1)], swap_sem.at[3])


def finish_kernel(
    land_hbm, give_hbm, state_hbm, tend_hbm, final_hbm, land, give, state, tend, in_sem, out_sem
):
    fields, levels = state.shape[:2]
    groups, cap, rows = land.shape
    small = [
        pltpu.make_async_copy(land_hbm, land, in_sem.at[0]),
        pltpu.make_async_copy(give_hbm, give, in_sem.at[1]),
    ]
    half = levels // 2
    pieces = [(f, pl.ds(i * half, half + i * (levels % 2))) for f in range(fields) for i in range(2)]
    ins = [
        pltpu.make_async_copy(state_hbm.at[f, z], state.at[f, z], in_sem.at[2 + i])
        for i, (f, z) in enumerate(pieces)
    ]
    stores = [
        pltpu.make_async_copy(state.at[f, z], final_hbm.at[f, z], out_sem.at[i])
        for i, (f, z) in enumerate(pieces)
    ]
    for copy in small + ins:
        copy.start()
    for copy in small:
        copy.wait()
    split = parts_of(land[...].reshape(groups * cap, rows))
    hot = give[...].astype(jnp.bfloat16)
    for load, store in zip(ins, stores):
        load.wait()
        store.start()
    back = pick(split, hot, ((0,), (0,)))
    tend[...] = back[: tend.shape[0]]
    store = pltpu.make_async_copy(tend, tend_hbm, out_sem.at[len(pieces)])
    store.start()
    for copy in stores + [store]:
        copy.wait()


def on_device(profiles, courant, owner_map, cloud_flags, crm_state):
    columns = profiles.shape[0]
    fields, levels, cells = crm_state.shape[:3]
    groups = lax.axis_size("col")
    peers = lax.axis_size("grp")
    per_peer = columns // groups
    cap = round_up(per_peer + min(2, per_peer), 8)
    chunks = columns // LANES
    direct = cells % 8 == 0
    reach = 1 if direct else DEPTH // cells
    full, edges = level_edges(levels)
    split = (full - 1) * BLOCK
    rows = round_up(fields * levels, 8 * peers)
    early_rows = round_up(fields * split, 8 * peers)
    late_rows = round_up(fields * (levels - split), 8)
    f32 = lambda *shape: pltpu.VMEM(shape, jnp.float32)
    i32 = lambda *shape: pltpu.VMEM(shape, jnp.int32)
    dma = lambda *shape: pltpu.SemaphoreType.DMA(shape)
    anywhere = pl.BlockSpec(memory_space=pl.ANY)
    tall = round_up(TOP + cells + 2 * DEPTH + 1, 8)
    slabs = (8, 128) if direct else (chunks, 2 * reach + 1, fields, levels, cells, LANES)
    land, give, state = pl.pallas_call(
        window_kernel,
        out_shape=(
            jax.ShapeDtypeStruct((groups, cap, rows), jnp.float32),
            jax.ShapeDtypeStruct((groups * cap, columns), jnp.float32),
            jax.ShapeDtypeStruct(crm_state.shape, jnp.float32),
        ),
        in_specs=[anywhere] * 5,
        out_specs=(anywhere,) * 3,
        scratch_shapes=[
            f32(fields * levels, columns),
            f32(levels, columns),
            i32(groups * chunks, LANES),
            i32(1, columns),
            f32(chunks, fields, levels, tall, LANES),
            f32(*slabs),
            f32(fields, levels, tall, LANES),
            f32(fields, levels, tall, LANES),
            f32(fields, levels, cells, columns),
            f32(groups * cap, columns),
            f32(groups * cap, columns),
            f32(groups, cap, 2 * LANES),
            f32(groups, cap, 2 * LANES),
            f32(chunks, 8, levels, LANES),
            f32(chunks, rows, LANES),
            f32(early_rows, LANES),
            f32(late_rows, LANES),
            f32(chunks, peers - 1, rows // peers, LANES),
            f32(peers - 1, early_rows // peers, LANES),
            f32(peers - 1, late_rows, LANES),
            f32(chunks, rows // peers, LANES),
            f32(early_rows // peers, LANES),
            f32(chunks, rows, LANES),
            f32(early_rows, LANES),
            f32(groups, cap, rows),
            dma(chunks + 4),
            dma(3),
            dma(1),
            dma(chunks, len(edges) - 1),
            dma(4),
            dma(2 * chunks + 1, 2),
        ],
        compiler_params=pltpu.CompilerParams(
            collective_id=0, has_side_effects=True, vmem_limit_bytes=LIMIT
        ),
    )(
        profiles.T,
        courant.T,
        owner_map.reshape(groups * chunks, LANES),
        cloud_flags[None, :],
        crm_state,
    )
    tendency, final = pl.pallas_call(
        finish_kernel,
        out_shape=(
            jax.ShapeDtypeStruct((fields * levels, columns), jnp.float32),
            jax.ShapeDtypeStruct(crm_state.shape, jnp.float32),
        ),
        in_specs=[anywhere] * 3,
        out_specs=(anywhere,) * 2,
        scratch_shapes=[
            f32(groups, cap, rows),
            f32(groups * cap, columns),
            f32(*crm_state.shape),
            f32(fields * levels, columns),
            dma(2 + 2 * fields),
            dma(1 + 2 * fields),
        ],
        compiler_params=pltpu.CompilerParams(vmem_limit_bytes=LIMIT),
    )(land, give, state)
    return tendency.T, final


def solution(mesh):
    placed = (P("col", None), P("col", None), P(), P("col"), P(None, None, "grp", "col"))
    return jax.shard_map(
        on_device,
        mesh=mesh,
        in_specs=placed,
        out_specs=(P("col", None), P(None, None, "grp", "col")),
        check_vma=False,
    )
```

time: 70.3 us -> 62.7 us (0.89)
  Pallas kernels: 66.3 us -> 61.9 us
  local copies, waits for them, and re-layouts: 3.11 us -> 0 us
    pallas_call x1, Pallas kernels: 64.4 us -> 59.2 us  [on_device(): pl.pallas_call(window_kernel, out_shape=(jax.ShapeDtypeStruct((groups, ca...]
    unnamed x8 -> x0, local copies, waits for them, and re-layouts: 3.11 us -> none
    pallas_call x1, Pallas kernels: 1.93 us -> 2.69 us  [on_device(): pl.pallas_call(finish_kernel, out_shape=(jax.ShapeDtypeStruct((fields * l...]
where the time goes in v2:
time: 62.7 us; the launch traced here: 62.5 us
  Pallas kernels  61.9 us (99%)
  between operations  0.64 us (1%)
    pallas_call x1, Pallas kernels, on_device(): pl.pallas_call(window_kernel, out_shape=(jax.ShapeDtypeStruct((groups, ca...  59.2 us
    pallas_call x1, Pallas kernels, on_device(): pl.pallas_call(finish_kernel, out_shape=(jax.ShapeDtypeStruct((fields * l...  2.69 us

profile of v2, /device:TPU:0, one launch (start us, length us, event | category | flops | bytes accessed | tf_op | source)
XLA Modules:
  0.0 62.5 jit_solution(1734351370556068715)
XLA Ops:
  0.6 59.2 %shard_map.68 = (f32[8,40,128]{2,1,0:T(8,128)}, f32[320,256]{1,0:T(8,128)}, f32[2,58,16,256]{3,2,1,0:T(8,128)}) custom-call(f32[116,256]{1,0:T(8,128)} %bitcast.5, f32[58,256]{1,0:T(8,128)} %bitcast.6, s32[16,128]{1,0:T(8,128)} %bitcast.7, s32[1,256]{1,0:T(1,128)} %bitcast.8, f32[2,58,16,256]{3,2,1,0:T(8,128)} %x_hbm.1), custom_call_target="tpu_custom_call" | custom-call | tf_op jit(solution)/shard_map/pallas_call | solution.py:524
  59.8 2.7 %shard_map.69 = (f32[116,256]{1,0:T(8,128)}, f32[2,58,16,256]{3,2,1,0:T(8,128)}) custom-call(f32[8,40,128]{2,1,0:T(8,128)} %get-tuple-element.7.land_hbm, f32[320,256]{1,0:T(8,128)} %get-tuple-element.8.give_hbm, f32[2,58,16,256]{3,2,1,0:T(8,128)} %get-tuple-element.9.state_hbm), custom_call_target="tpu_custom_call" | custom-call | tf_op jit(solution)/shard_map/pallas_call | solution.py:576

commit v3 on v2

--- a/solution.py
+++ b/solution.py
@@ -9,6 +9,10 @@
 DEPTH = STEPS
 BLOCK = 8
 PIECE = 4
+AHEAD = 3
+LEAD = 3
+HELD = -1
+PIECES = 2
 LANES = 128
 LIMIT = 67_043_328
 TOP = 8
@@ -42,6 +46,14 @@
             *pair, (dims, ((), ())), preferred_element_type=jnp.float32
         )
     return total
+
+
+def flip(index, mask):
+    place = index
+    for i in range(mask.bit_length()):
+        if mask >> i & 1:
+            place = place + (1 << i) - (2 << i) * lax.rem(lax.div(index, 1 << i), 2)
+    return place
 
 
 def level_edges(levels):
@@ -92,6 +104,7 @@
     halo_recv,
     swap_sem,
     sum_sem,
+    meet,
 ):
     fields, levels, cells, columns = x_hbm.shape
     chunks = columns // LANES
@@ -104,7 +117,7 @@
     width = cells + 2 * DEPTH
     own = TOP + DEPTH
     full, edges = level_edges(levels)
-    split = (full - 1) * BLOCK
+    split = edges[full + HELD] - BLOCK
     span = lambda i: pl.ds(i * LANES, LANES)
 
     loads = []
@@ -123,16 +136,6 @@
         load.start()
         small.append(load)
 
-    barrier = pltpu.get_barrier_semaphore()
-    for k in range(1, peers):
-        pl.semaphore_signal(
-            barrier, inc=1, device_id={"grp": lax.rem(z_me + k, peers)}, device_id_type=MESH
-        )
-    for k in range(1, groups):
-        pl.semaphore_signal(
-            barrier, inc=1, device_id={"col": lax.rem(c_me + k, groups)}, device_id_type=MESH
-        )
-
     def remote(source, target, send, recv, axis, peer):
         return pltpu.make_async_remote_copy(
             src_ref=source,
@@ -149,28 +152,114 @@
     def sent(ref, sem):
         remote(ref, ref, sem, sem, "grp", z_me).wait_send()
 
-    def send_halos(c, b):
+    def send_slabs(c, b):
         rows = pl.ds(edges[b], edges[b + 1] - edges[b])
         for j in range(1, reach + 1):
             for side in range(2):
                 peer = lax.rem(z_me + (peers - j if side == 0 else j), peers)
-                if direct:
-                    near = own if side == 0 else own + cells - DEPTH
-                    far = own + cells if side == 0 else TOP
-                    source = wide.at[c, :, rows, near : near + DEPTH, :]
-                    target = wide.at[c, :, rows, far : far + DEPTH, :]
-                else:
-                    source = slabs.at[c, 2 * reach, :, rows]
-                    target = slabs.at[c, 2 * (j - 1) + side, :, rows]
+                source = slabs.at[c, 2 * reach, :, rows]
+                target = slabs.at[c, 2 * (j - 1) + side, :, rows]
                 remote(source, target, halo_send.at[0], halo_recv.at[c, b], "grp", peer).start()
 
-    with jax.named_scope("barrier"):
+    lead = jnp.where(z_me == peers - 1, 1, 0)
+    items = [(c, b) for c in range(chunks) for b in range(len(edges) - 1)]
+
+    def send_rows(i, side):
+        c, b = items[i]
+        rows = pl.ds(edges[b], edges[b + 1] - edges[b])
+        peer = lax.rem(z_me + side + (1 - side) * (peers - 1), peers)
+        near = pl.multiple_of(own + side * (cells - DEPTH), 8)
+        far = pl.multiple_of(own + cells - side * (cells + DEPTH), 8)
+        source = wide.at[c, :, rows, pl.ds(near, DEPTH), :]
+        target = wide.at[c, :, rows, pl.ds(far, DEPTH), :]
+        remote(source, target, halo_send.at[0], halo_recv.at[c, b], "grp", peer).start()
+
+    barrier = pltpu.get_barrier_semaphore()
+
+    def signal(sem, axis, peer):
+        pl.semaphore_signal(sem, inc=1, device_id={axis: peer}, device_id_type=MESH)
+
+    if direct and peers > 2 and groups & (groups - 1) == 0:
+        at_left, at_right = z_me == 0, z_me == peers - 1
+        ends = at_left | at_right
+        bits = [1 << i for i in range(groups.bit_length() - 1)]
+        across = [flip(c_me, k) for k in bits]
+
+        @pl.when(z_me > 0)
+        def _():
+            signal(barrier, "grp", z_me - 1)
+
+        @pl.when(z_me < peers - 1)
+        def _():
+            signal(barrier, "grp", z_me + 1)
+
+        for peer in across:
+            signal(barrier, "col", peer)
+        with jax.named_scope("barrier"):
+            pl.semaphore_wait(barrier, len(bits) + 2 - jnp.where(ends, 1, 0))
+        with jax.named_scope("send"):
+            loads[0].wait()
+            for i in range(AHEAD):
+                send_rows(i, 1 - lead)
+
+            @pl.when(jnp.logical_not(ends))
+            def _():
+                for i in range(AHEAD):
+                    send_rows(i, lead)
+
+            @pl.when((z_me > 0) & (z_me < peers - 1))
+            def _():
+                signal(meet.at[0], "grp", z_me - 1)
+                signal(meet.at[1], "grp", z_me + 1)
+
+            for r in range(peers - 2):
+
+                @pl.when(r < peers - 2 - z_me)
+                def _():
+                    pl.semaphore_wait(meet.at[0], 1)
+
+                    @pl.when(z_me > 0)
+                    def _():
+                        signal(meet.at[0], "grp", z_me - 1)
+
+                @pl.when(r < z_me - 1)
+                def _():
+                    pl.semaphore_wait(meet.at[1], 1)
+
+                    @pl.when(z_me < peers - 1)
+                    def _():
+                        signal(meet.at[1], "grp", z_me + 1)
+
+            @pl.when(ends)
+            def _():
+                for i in range(AHEAD):
+                    send_rows(i, lead)
+
+            for load in loads[1:]:
+                load.wait()
+            for i in range(AHEAD, AHEAD + LEAD):
+                send_rows(i, lead)
+            for i in range(AHEAD, len(items)):
+                send_rows(i, 1 - lead)
+                if i + LEAD < len(items):
+                    send_rows(i + LEAD, lead)
+            for i, peer in enumerate(across[1:]):
+                signal(meet.at[2 + i], "col", peer)
+                pl.semaphore_wait(meet.at[2 + i], 1)
+    else:
+        for k in range(1, peers):
+            signal(barrier, "grp", lax.rem(z_me + k, peers))
+        for k in range(1, groups):
+            signal(barrier, "col", lax.rem(c_me + k, groups))
         pl.semaphore_wait(barrier, peers - 1 + groups - 1)
-    with jax.named_scope("send"):
-        for c in range(chunks):
-            loads[c].wait()
-            for b in range(len(edges) - 1):
-                send_halos(c, b)
+        for load in loads:
+            load.wait()
+        for i, (c, b) in enumerate(items):
+            if direct:
+                send_rows(i, 0)
+                send_rows(i, 1)
+            else:
+                send_slabs(c, b)
 
     with jax.named_scope("forcing"):
         for load in small:
@@ -329,7 +418,7 @@
 
             lax.fori_loop(start, start + count, fill, 0)
 
-    def opening(c, sums, row):
+    def opening(c, sums, row, stop):
         with jax.named_scope(f"first#c={c}"):
             arrive(c, 0, 0, BLOCK)
             for s in range(1, STEPS + 1):
@@ -343,7 +432,7 @@
                     sweep(c, s, b * BLOCK - s, BLOCK, sums, row, 4)
             return carry
 
-        lax.fori_loop(1, full, body, 0)
+        lax.fori_loop(1, stop, body, 0)
 
     def scatter(part, landing, sem):
         lines = part.shape[0] // peers
@@ -372,7 +461,7 @@
     for c in range(last):
         whole[c, fields * levels :, :] = jnp.zeros_like(whole[c, fields * levels :, :])
         row = lambda f, z: f * levels + z
-        opening(c, whole.at[c], row)
+        opening(c, whole.at[c], row, full)
         for b in range(full, len(edges) - 1):
             arrive(c, b, edges[b], edges[b + 1] - edges[b])
         with jax.named_scope("closing"):
@@ -382,29 +471,33 @@
         pltpu.make_async_copy(
             outs.at[:, :, :, span(c)], final_hbm.at[:, :, :, span(c)], out_sem.at[1]
         ).start()
-    early[fields * split :, :] = jnp.zeros_like(early[fields * split :, :])
-    late[fields * (levels - split) :, :] = jnp.zeros_like(late[fields * (levels - split) :, :])
-    opening(last, early, lambda f, z: f * split + z)
-    scatter(early, early_heap, sum_sem.at[2 * last])
-    pltpu.make_async_copy(
-        outs.at[:, pl.ds(0, split), :, span(last)],
-        final_hbm.at[:, pl.ds(0, split), :, span(last)],
-        out_sem.at[1],
-    ).start()
-    row = lambda f, z: f * (levels - split) + z - split
-    for b in range(full, len(edges) - 1):
+    if early.shape[0] > fields * split:
+        early[fields * split :, :] = jnp.zeros_like(early[fields * split :, :])
+    if late.shape[0] > fields * (levels - split):
+        late[fields * (levels - split) :, :] = jnp.zeros_like(late[fields * (levels - split) :, :])
+    early_row = lambda f, z: f * split + z
+    late_row = lambda f, z: f * (levels - split) + z - split
+    pause = full + min(HELD, 0)
+    opening(last, early, early_row, pause)
+    for b in range(pause, len(edges) - 1):
+        if b == full + HELD:
+            scatter(early, early_heap, sum_sem.at[2 * last])
+            pltpu.make_async_copy(
+                outs.at[:, pl.ds(0, split), :, span(last)],
+                final_hbm.at[:, pl.ds(0, split), :, span(last)],
+                out_sem.at[1],
+            ).start()
         with jax.named_scope(f"late_arrive#b={b}"):
             arrive(last, b, edges[b], edges[b + 1] - edges[b])
         with jax.named_scope(f"late_steps#b={b}"):
             ends = b == len(edges) - 2
+            sums, row = (early, early_row) if b < full + HELD else (late, late_row)
             for s in range(1, STEPS + 1):
                 count = edges[b + 1] - edges[b] + (s if ends else 0)
-                sweep(last, s, edges[b] - s, count, late, row, count if ends else 4)
+                sweep(last, s, edges[b] - s, count, sums, row, count if ends else 4)
+    late_sem = sum_sem.at[2 * chunks]
     for k in range(1, peers):
-        peer = lax.rem(z_me + k, peers)
-        remote(
-            late, late_heap.at[k - 1], sum_sem.at[2 * last + 2, 0], sum_sem.at[2 * last + 2, 1], "grp", peer
-        ).start()
+        remote(late, late_heap.at[k - 1], late_sem.at[0], late_sem.at[1], "grp", flip(z_me, k)).start()
     pltpu.make_async_copy(
         outs.at[:, pl.ds(split, levels - split), :, span(last)],
         final_hbm.at[:, pl.ds(split, levels - split), :, span(last)],
@@ -415,12 +508,12 @@
             gather(whole.at[c], heap.at[c], mine.at[c], inc.at[c], sum_sem.at[2 * c], sum_sem.at[2 * c + 1])
         gather(early, early_heap, early_mine, early_inc, sum_sem.at[2 * last], sum_sem.at[2 * last + 1])
     with jax.named_scope("late_wait"):
-        received(late_heap, sum_sem.at[2 * last + 2, 1])
-        total = late[...]
-        for k in range(peers - 1):
-            total = total + late_heap[k]
+        received(late_heap, late_sem.at[1])
+        totals = [late[...]] + [late_heap[k] for k in range(peers - 1)]
+        while len(totals) > 1:
+            totals = [x + y for x, y in zip(totals[::2], totals[1::2])]
         for f in range(fields):
-            inc[last, f * levels + split : (f + 1) * levels, :] = total[
+            inc[last, f * levels + split : (f + 1) * levels, :] = totals[0][
                 f * (levels - split) : (f + 1) * (levels - split)
             ]
         inc[last, fields * levels :, :] = jnp.zeros_like(inc[last, fields * levels :, :])
@@ -439,8 +532,8 @@
             parts_of(inc[last]), hot[:, last * LANES :], ((1,), (1,)), swap=True
         )
         pack[...] = (packed / (cells * peers)).reshape(pack.shape)
-    for k in range(1, groups):
-        peer = lax.rem(c_me + k, groups)
+    for k in sorted(range(1, groups), key=lambda k: -bin(k >> 1).count("1")):
+        peer = flip(c_me, k)
         remote(pack.at[peer], land.at[c_me], swap_sem.at[2], swap_sem.at[3], "col", peer).start()
     keep = pltpu.make_async_copy(pack.at[c_me], land.at[c_me], out_sem.at[2])
     keep.start()
@@ -455,7 +548,7 @@
             sent(others(inc.at[c]), sum_sem.at[2 * c + 1, 0])
         sent(others(early_inc), sum_sem.at[2 * last, 0])
         sent(others(early_inc), sum_sem.at[2 * last + 1, 0])
-        sent(late_heap, sum_sem.at[2 * last + 2, 0])
+        sent(late_heap, late_sem.at[0])
         give_out.wait()
         pltpu.make_async_copy(outs, final_hbm, out_sem.at[1]).wait()
         keep.wait()
@@ -473,8 +566,8 @@
         pltpu.make_async_copy(land_hbm, land, in_sem.at[0]),
         pltpu.make_async_copy(give_hbm, give, in_sem.at[1]),
     ]
-    half = levels // 2
-    pieces = [(f, pl.ds(i * half, half + i * (levels % 2))) for f in range(fields) for i in range(2)]
+    cuts = [levels * i // PIECES for i in range(PIECES + 1)]
+    pieces = [(f, pl.ds(a, b - a)) for f in range(fields) for a, b in zip(cuts, cuts[1:])]
     ins = [
         pltpu.make_async_copy(state_hbm.at[f, z], state.at[f, z], in_sem.at[2 + i])
         for i, (f, z) in enumerate(pieces)
@@ -511,7 +604,7 @@
     direct = cells % 8 == 0
     reach = 1 if direct else DEPTH // cells
     full, edges = level_edges(levels)
-    split = (full - 1) * BLOCK
+    split = edges[full + HELD] - BLOCK
     rows = round_up(fields * levels, 8 * peers)
     early_rows = round_up(fields * split, 8 * peers)
     late_rows = round_up(fields * (levels - split), 8)
@@ -562,6 +655,7 @@
             dma(chunks, len(edges) - 1),
             dma(4),
             dma(2 * chunks + 1, 2),
+            pltpu.SemaphoreType.REGULAR((max(2, groups.bit_length()),)),
         ],
         compiler_params=pltpu.CompilerParams(
             collective_id=0, has_side_effects=True, vmem_limit_bytes=LIMIT
@@ -586,8 +680,8 @@
             f32(groups * cap, columns),
             f32(*crm_state.shape),
             f32(fields * levels, columns),
-            dma(2 + 2 * fields),
-            dma(1 + 2 * fields),
+            dma(2 + PIECES * fields),
+            dma(1 + PIECES * fields),
         ],
         compiler_params=pltpu.CompilerParams(vmem_limit_bytes=LIMIT),
     )(land, give, state)

time: 62.7 us -> 62.3 us (level)
  no operation moved by 1% of the time
where the time goes in v3:
time: 62.3 us; the launch traced here: 62.2 us
  Pallas kernels  61.5 us (99%)
  between operations  0.64 us (1%)
    pallas_call x1, Pallas kernels, on_device(): pl.pallas_call(window_kernel, out_shape=(jax.ShapeDtypeStruct((groups, ca...  58.8 us
    pallas_call x1, Pallas kernels, on_device(): pl.pallas_call(finish_kernel, out_shape=(jax.ShapeDtypeStruct((fields * l...  2.69 us

profile of v3, /device:TPU:0, one launch (start us, length us, event | category | flops | bytes accessed | tf_op | source)
XLA Modules:
  0.0 62.2 jit_solution(12852484976613098589)
XLA Ops:
  0.6 58.8 %shard_map.68 = (f32[8,40,128]{2,1,0:T(8,128)}, f32[320,256]{1,0:T(8,128)}, f32[2,58,16,256]{3,2,1,0:T(8,128)}) custom-call(f32[116,256]{1,0:T(8,128)} %bitcast.5, f32[58,256]{1,0:T(8,128)} %bitcast.6, s32[16,128]{1,0:T(8,128)} %bitcast.7, s32[1,256]{1,0:T(1,128)} %bitcast.8, f32[2,58,16,256]{3,2,1,0:T(8,128)} %x_hbm.1), custom_call_target="tpu_custom_call" | custom-call | tf_op jit(solution)/shard_map/pallas_call | solution.py:617
  59.5 2.7 %shard_map.69 = (f32[116,256]{1,0:T(8,128)}, f32[2,58,16,256]{3,2,1,0:T(8,128)}) custom-call(f32[8,40,128]{2,1,0:T(8,128)} %get-tuple-element.7.land_hbm, f32[320,256]{1,0:T(8,128)} %get-tuple-element.8.give_hbm, f32[2,58,16,256]{3,2,1,0:T(8,128)} %get-tuple-element.9.state_hbm), custom_call_target="tpu_custom_call" | custom-call | tf_op jit(solution)/shard_map/pallas_call | solution.py:670

commit v4 on v3

--- a/solution.py
+++ b/solution.py
@@ -9,9 +9,8 @@
 DEPTH = STEPS
 BLOCK = 8
 PIECE = 4
-AHEAD = 3
-LEAD = 3
-HELD = -1
+AHEAD = 2
+LEAD = 1
 PIECES = 2
 LANES = 128
 LIMIT = 67_043_328
@@ -46,6 +45,13 @@
             *pair, (dims, ((), ())), preferred_element_type=jnp.float32
         )
     return total
+
+
+def split_level(fields, levels, chunks, peers, limit):
+    for split in range(limit, 0, -1):
+        if fields * (levels * (chunks - 1) + split) % (8 * peers) == 0:
+            return split
+    return limit
 
 
 def flip(index, mask):
@@ -87,16 +93,13 @@
     fsend,
     fland,
     coef,
-    whole,
-    early,
+    bulk,
     late,
     heap,
-    early_heap,
     late_heap,
     mine,
-    early_mine,
+    summed,
     inc,
-    early_inc,
     pack,
     load_sem,
     out_sem,
@@ -117,7 +120,8 @@
     width = cells + 2 * DEPTH
     own = TOP + DEPTH
     full, edges = level_edges(levels)
-    split = edges[full + HELD] - BLOCK
+    split = split_level(fields, levels, chunks, peers, edges[full] - BLOCK)
+    kept = fields * levels * (chunks - 1)
     span = lambda i: pl.ds(i * LANES, LANES)
 
     loads = []
@@ -367,7 +371,20 @@
             moisture = moisture - sat_scale
         return first, rows, (energy, moisture)
 
-    def put(c, s, z, result, sums, row):
+    def keep_row(f, z, total):
+        def early():
+            bulk[pl.ds(kept + f * split + z, 1), :] = total
+
+        def later():
+            late[pl.ds(f * (levels - split) + z - split, 1), :] = total
+
+        if isinstance(z, int):
+            (early if z < split else later)()
+        else:
+            pl.when(z < split)(early)
+            pl.when(z >= split)(later)
+
+    def put(c, s, z, result):
         first, rows, values = result
         target = odd if s % 2 else even
         for f, value in enumerate(values):
@@ -377,16 +394,20 @@
                     old = wide[c, f, z, own : own + cells]
                 else:
                     old = slabs[c, 2 * reach, f, z]
-                sums[pl.ds(row(f, z), 1), :] = jnp.sum(value - old, axis=0, keepdims=True)
+                total = jnp.sum(value - old, axis=0, keepdims=True)
+                if c < chunks - 1:
+                    bulk[pl.ds((c * fields + f) * levels + z, 1), :] = total
+                else:
+                    keep_row(f, z, total)
             else:
                 target[f, z, first : first + rows] = value
 
-    def sweep(c, s, low, count, sums, row, unroll):
+    def sweep(c, s, low, count, unroll):
         def body(i, carry):
             z = low + unroll * i
             results = [stepped(c, s, z + k) for k in range(unroll)]
             for k in range(unroll):
-                put(c, s, z + k, results[k], sums, row)
+                put(c, s, z + k, results[k])
             return carry
 
         trips = count // unroll
@@ -397,7 +418,7 @@
         rest = [low + k for k in range(trips * unroll, count)]
         results = [stepped(c, s, z) for z in rest]
         for z, result in zip(rest, results):
-            put(c, s, z, result, sums, row)
+            put(c, s, z, result)
 
     def arrive(c, b, start, count):
         rows = pl.ds(start, count)
@@ -418,18 +439,18 @@
 
             lax.fori_loop(start, start + count, fill, 0)
 
-    def opening(c, sums, row, stop):
+    def opening(c, stop):
         with jax.named_scope(f"first#c={c}"):
             arrive(c, 0, 0, BLOCK)
             for s in range(1, STEPS + 1):
-                sweep(c, s, 0, BLOCK - s, sums, row, 2)
+                sweep(c, s, 0, BLOCK - s, 2)
 
         def body(b, carry):
             with jax.named_scope("arrive"):
                 arrive(c, b, b * BLOCK, BLOCK)
             with jax.named_scope("steps"):
                 for s in range(1, STEPS + 1):
-                    sweep(c, s, b * BLOCK - s, BLOCK, sums, row, 4)
+                    sweep(c, s, b * BLOCK - s, BLOCK, 4)
             return carry
 
         lax.fori_loop(1, stop, body, 0)
@@ -458,55 +479,47 @@
         return ref.at[pl.ds(0, ref.shape[0] // peers * (peers - 1))]
 
     last = chunks - 1
+    if bulk.shape[0] > kept + fields * split:
+        bulk[kept + fields * split :, :] = jnp.zeros_like(bulk[kept + fields * split :, :])
+    if late.shape[0] > fields * (levels - split):
+        late[fields * (levels - split) :, :] = jnp.zeros_like(late[fields * (levels - split) :, :])
     for c in range(last):
-        whole[c, fields * levels :, :] = jnp.zeros_like(whole[c, fields * levels :, :])
-        row = lambda f, z: f * levels + z
-        opening(c, whole.at[c], row, full)
+        opening(c, full)
         for b in range(full, len(edges) - 1):
             arrive(c, b, edges[b], edges[b + 1] - edges[b])
         with jax.named_scope("closing"):
             for s in range(1, STEPS + 1):
-                sweep(c, s, edges[full] - s, levels - edges[full] + s, whole.at[c], row, 2)
-        scatter(whole.at[c], heap.at[c], sum_sem.at[2 * c])
+                sweep(c, s, edges[full] - s, levels - edges[full] + s, 2)
         pltpu.make_async_copy(
             outs.at[:, :, :, span(c)], final_hbm.at[:, :, :, span(c)], out_sem.at[1]
         ).start()
-    if early.shape[0] > fields * split:
-        early[fields * split :, :] = jnp.zeros_like(early[fields * split :, :])
-    if late.shape[0] > fields * (levels - split):
-        late[fields * (levels - split) :, :] = jnp.zeros_like(late[fields * (levels - split) :, :])
-    early_row = lambda f, z: f * split + z
-    late_row = lambda f, z: f * (levels - split) + z - split
-    pause = full + min(HELD, 0)
-    opening(last, early, early_row, pause)
-    for b in range(pause, len(edges) - 1):
-        if b == full + HELD:
-            scatter(early, early_heap, sum_sem.at[2 * last])
+    ready = edges[full] - BLOCK
+    opening(last, full)
+    for b in range(full, len(edges) - 1):
+        if b == full:
+            scatter(bulk, heap, sum_sem.at[0])
             pltpu.make_async_copy(
-                outs.at[:, pl.ds(0, split), :, span(last)],
-                final_hbm.at[:, pl.ds(0, split), :, span(last)],
+                outs.at[:, pl.ds(0, ready), :, span(last)],
+                final_hbm.at[:, pl.ds(0, ready), :, span(last)],
                 out_sem.at[1],
             ).start()
         with jax.named_scope(f"late_arrive#b={b}"):
             arrive(last, b, edges[b], edges[b + 1] - edges[b])
         with jax.named_scope(f"late_steps#b={b}"):
             ends = b == len(edges) - 2
-            sums, row = (early, early_row) if b < full + HELD else (late, late_row)
             for s in range(1, STEPS + 1):
                 count = edges[b + 1] - edges[b] + (s if ends else 0)
-                sweep(last, s, edges[b] - s, count, sums, row, count if ends else 4)
-    late_sem = sum_sem.at[2 * chunks]
-    for k in range(1, peers):
+                sweep(last, s, edges[b] - s, count, count if ends else 4)
+    late_sem = sum_sem.at[2]
+    for k in range(peers - 1, 0, -1):
         remote(late, late_heap.at[k - 1], late_sem.at[0], late_sem.at[1], "grp", flip(z_me, k)).start()
     pltpu.make_async_copy(
-        outs.at[:, pl.ds(split, levels - split), :, span(last)],
-        final_hbm.at[:, pl.ds(split, levels - split), :, span(last)],
+        outs.at[:, pl.ds(ready, levels - ready), :, span(last)],
+        final_hbm.at[:, pl.ds(ready, levels - ready), :, span(last)],
         out_sem.at[1],
     ).start()
     with jax.named_scope("scatter_wait"):
-        for c in range(last):
-            gather(whole.at[c], heap.at[c], mine.at[c], inc.at[c], sum_sem.at[2 * c], sum_sem.at[2 * c + 1])
-        gather(early, early_heap, early_mine, early_inc, sum_sem.at[2 * last], sum_sem.at[2 * last + 1])
+        gather(bulk, heap, mine, summed, sum_sem.at[0], sum_sem.at[1])
     with jax.named_scope("late_wait"):
         received(late_heap, late_sem.at[1])
         totals = [late[...]] + [late_heap[k] for k in range(peers - 1)]
@@ -517,20 +530,22 @@
                 f * (levels - split) : (f + 1) * (levels - split)
             ]
         inc[last, fields * levels :, :] = jnp.zeros_like(inc[last, fields * levels :, :])
+        for c in range(last):
+            inc[c, fields * levels :, :] = jnp.zeros_like(inc[c, fields * levels :, :])
     with jax.named_scope("gather_wait"):
+        received(others(summed), sum_sem.at[1, 1])
+    with jax.named_scope("pack"):
+        for c in range(last):
+            start = c * fields * levels
+            inc[c, : fields * levels, :] = summed[start : start + fields * levels, :]
+        for f in range(fields):
+            start = kept + f * split
+            inc[last, f * levels : f * levels + split, :] = summed[start : start + split, :]
         packed = 0.0
-        for c in range(last):
-            received(others(inc.at[c]), sum_sem.at[2 * c + 1, 1])
+        for c in range(chunks):
             packed = packed + pick(
                 parts_of(inc[c]), hot[:, c * LANES : (c + 1) * LANES], ((1,), (1,)), swap=True
             )
-        received(others(early_inc), sum_sem.at[2 * last + 1, 1])
-    with jax.named_scope("pack"):
-        for f in range(fields):
-            inc[last, f * levels : f * levels + split, :] = early_inc[f * split : (f + 1) * split, :]
-        packed = packed + pick(
-            parts_of(inc[last]), hot[:, last * LANES :], ((1,), (1,)), swap=True
-        )
         pack[...] = (packed / (cells * peers)).reshape(pack.shape)
     for k in sorted(range(1, groups), key=lambda k: -bin(k >> 1).count("1")):
         peer = flip(c_me, k)
@@ -543,11 +558,8 @@
         else:
             sent(slabs.at[:, pl.ds(0, 2 * reach)], halo_send.at[0])
         sent(fsend.at[pl.ds(0, groups - 1)], swap_sem.at[0])
-        for c in range(last):
-            sent(others(inc.at[c]), sum_sem.at[2 * c, 0])
-            sent(others(inc.at[c]), sum_sem.at[2 * c + 1, 0])
-        sent(others(early_inc), sum_sem.at[2 * last, 0])
-        sent(others(early_inc), sum_sem.at[2 * last + 1, 0])
+        sent(others(summed), sum_sem.at[0, 0])
+        sent(others(summed), sum_sem.at[1, 0])
         sent(late_heap, late_sem.at[0])
         give_out.wait()
         pltpu.make_async_copy(outs, final_hbm, out_sem.at[1]).wait()
@@ -604,9 +616,9 @@
     direct = cells % 8 == 0
     reach = 1 if direct else DEPTH // cells
     full, edges = level_edges(levels)
-    split = edges[full + HELD] - BLOCK
-    rows = round_up(fields * levels, 8 * peers)
-    early_rows = round_up(fields * split, 8 * peers)
+    split = split_level(fields, levels, chunks, peers, edges[full] - BLOCK)
+    rows = round_up(fields * levels, LANES)
+    bulk_rows = round_up(fields * (levels * (chunks - 1) + split), 8 * peers)
     late_rows = round_up(fields * (levels - split), 8)
     f32 = lambda *shape: pltpu.VMEM(shape, jnp.float32)
     i32 = lambda *shape: pltpu.VMEM(shape, jnp.int32)
@@ -638,23 +650,20 @@
             f32(groups, cap, 2 * LANES),
             f32(groups, cap, 2 * LANES),
             f32(chunks, 8, levels, LANES),
+            f32(bulk_rows, LANES),
+            f32(late_rows, LANES),
+            f32(peers - 1, bulk_rows // peers, LANES),
+            f32(peers - 1, late_rows, LANES),
+            f32(bulk_rows // peers, LANES),
+            f32(bulk_rows, LANES),
             f32(chunks, rows, LANES),
-            f32(early_rows, LANES),
-            f32(late_rows, LANES),
-            f32(chunks, peers - 1, rows // peers, LANES),
-            f32(peers - 1, early_rows // peers, LANES),
-            f32(peers - 1, late_rows, LANES),
-            f32(chunks, rows // peers, LANES),
-            f32(early_rows // peers, LANES),
-            f32(chunks, rows, LANES),
-            f32(early_rows, LANES),
             f32(groups, cap, rows),
             dma(chunks + 4),
             dma(3),
             dma(1),
             dma(chunks, len(edges) - 1),
             dma(4),
-            dma(2 * chunks + 1, 2),
+            dma(3, 2),
             pltpu.SemaphoreType.REGULAR((max(2, groups.bit_length()),)),
         ],
         compiler_params=pltpu.CompilerParams(

time: 62.3 us -> 61.9 us (level)
  no operation moved by 1% of the time
where the time goes in v4:
time: 61.9 us; the launch traced here: 61.7 us
  Pallas kernels  61.1 us (99%)
  between operations  0.64 us (1%)
    pallas_call x1, Pallas kernels, on_device(): pl.pallas_call(window_kernel, out_shape=(jax.ShapeDtypeStruct((groups, ca...  58.4 us
    pallas_call x1, Pallas kernels, on_device(): pl.pallas_call(finish_kernel, out_shape=(jax.ShapeDtypeStruct((fields * l...  2.69 us

profile of v4, /device:TPU:0, one launch (start us, length us, event | category | flops | bytes accessed | tf_op | source)
XLA Modules:
  0.0 61.7 jit_solution(1258101971364832104)
XLA Ops:
  0.6 58.4 %shard_map.68 = (f32[8,40,128]{2,1,0:T(8,128)}, f32[320,256]{1,0:T(8,128)}, f32[2,58,16,256]{3,2,1,0:T(8,128)}) custom-call(f32[116,256]{1,0:T(8,128)} %bitcast.5, f32[58,256]{1,0:T(8,128)} %bitcast.6, s32[16,128]{1,0:T(8,128)} %bitcast.7, s32[1,256]{1,0:T(1,128)} %bitcast.8, f32[2,58,16,256]{3,2,1,0:T(8,128)} %x_hbm.1), custom_call_target="tpu_custom_call" | custom-call | tf_op jit(solution)/shard_map/pallas_call | solution.py:629
  59.1 2.7 %shard_map.69 = (f32[116,256]{1,0:T(8,128)}, f32[2,58,16,256]{3,2,1,0:T(8,128)}) custom-call(f32[8,40,128]{2,1,0:T(8,128)} %get-tuple-element.7.land_hbm, f32[320,256]{1,0:T(8,128)} %get-tuple-element.8.give_hbm, f32[2,58,16,256]{3,2,1,0:T(8,128)} %get-tuple-element.9.state_hbm), custom_call_target="tpu_custom_call" | custom-call | tf_op jit(solution)/shard_map/pallas_call | solution.py:679

commit v5 on v4

--- a/solution.py
+++ b/solution.py
@@ -157,26 +157,30 @@
         remote(ref, ref, sem, sem, "grp", z_me).wait_send()
 
     def send_slabs(c, b):
-        rows = pl.ds(edges[b], edges[b + 1] - edges[b])
+        rows = pl.ds(edges[b], stop(c, b) - edges[b])
         for j in range(1, reach + 1):
             for side in range(2):
                 peer = lax.rem(z_me + (peers - j if side == 0 else j), peers)
                 source = slabs.at[c, 2 * reach, :, rows]
                 target = slabs.at[c, 2 * (j - 1) + side, :, rows]
-                remote(source, target, halo_send.at[0], halo_recv.at[c, b], "grp", peer).start()
+                remote(source, target, halo_send.at[0], landed_at(c, b), "grp", peer).start()
 
     lead = jnp.where(z_me == peers - 1, 1, 0)
-    items = [(c, b) for c in range(chunks) for b in range(len(edges) - 1)]
+    items = [
+        (c, b) for c in range(chunks) for b in range(full + 1 if c < chunks - 1 else len(edges) - 1)
+    ]
+    stop = lambda c, b: levels if c < chunks - 1 and b == full else edges[b + 1]
+    landed_at = lambda c, b: halo_recv.at[c * (full + 1) + b]
 
     def send_rows(i, side):
         c, b = items[i]
-        rows = pl.ds(edges[b], edges[b + 1] - edges[b])
+        rows = pl.ds(edges[b], stop(c, b) - edges[b])
         peer = lax.rem(z_me + side + (1 - side) * (peers - 1), peers)
         near = pl.multiple_of(own + side * (cells - DEPTH), 8)
         far = pl.multiple_of(own + cells - side * (cells + DEPTH), 8)
         source = wide.at[c, :, rows, pl.ds(near, DEPTH), :]
         target = wide.at[c, :, rows, pl.ds(far, DEPTH), :]
-        remote(source, target, halo_send.at[0], halo_recv.at[c, b], "grp", peer).start()
+        remote(source, target, halo_send.at[0], landed_at(c, b), "grp", peer).start()
 
     barrier = pltpu.get_barrier_semaphore()
 
@@ -423,9 +427,9 @@
     def arrive(c, b, start, count):
         rows = pl.ds(start, count)
         if direct:
-            received(wide.at[c, :, rows, TOP : TOP + 2 * DEPTH, :], halo_recv.at[c, b])
+            received(wide.at[c, :, rows, TOP : TOP + 2 * DEPTH, :], landed_at(c, b))
         else:
-            received(slabs.at[c, pl.ds(0, 2 * reach), :, rows], halo_recv.at[c, b])
+            received(slabs.at[c, pl.ds(0, 2 * reach), :, rows], landed_at(c, b))
 
             def fill(z, carry):
                 for f in range(fields):
@@ -485,8 +489,7 @@
         late[fields * (levels - split) :, :] = jnp.zeros_like(late[fields * (levels - split) :, :])
     for c in range(last):
         opening(c, full)
-        for b in range(full, len(edges) - 1):
-            arrive(c, b, edges[b], edges[b + 1] - edges[b])
+        arrive(c, full, edges[full], levels - edges[full])
         with jax.named_scope("closing"):
             for s in range(1, STEPS + 1):
                 sweep(c, s, edges[full] - s, levels - edges[full] + s, 2)
@@ -661,7 +664,7 @@
             dma(chunks + 4),
             dma(3),
             dma(1),
-            dma(chunks, len(edges) - 1),
+            dma((chunks - 1) * (full + 1) + len(edges) - 1),
             dma(4),
             dma(3, 2),
             pltpu.SemaphoreType.REGULAR((max(2, groups.bit_length()),)),

time: 61.9 us -> 61.9 us (level)
  no operation moved by 1% of the time
where the time goes in v5:
time: 61.9 us; the launch traced here: 61.7 us
  Pallas kernels  61.1 us (99%)
  between operations  0.64 us (1%)
    pallas_call x1, Pallas kernels, on_device(): pl.pallas_call(window_kernel, out_shape=(jax.ShapeDtypeStruct((groups, ca...  58.4 us
    pallas_call x1, Pallas kernels, on_device(): pl.pallas_call(finish_kernel, out_shape=(jax.ShapeDtypeStruct((fields * l...  2.69 us

profile of v5, /device:TPU:0, one launch (start us, length us, event | category | flops | bytes accessed | tf_op | source)
XLA Modules:
  0.0 61.7 jit_solution(9154553195347899904)
XLA Ops:
  0.6 58.4 %shard_map.68 = (f32[8,40,128]{2,1,0:T(8,128)}, f32[320,256]{1,0:T(8,128)}, f32[2,58,16,256]{3,2,1,0:T(8,128)}) custom-call(f32[116,256]{1,0:T(8,128)} %bitcast.5, f32[58,256]{1,0:T(8,128)} %bitcast.6, s32[16,128]{1,0:T(8,128)} %bitcast.7, s32[1,256]{1,0:T(1,128)} %bitcast.8, f32[2,58,16,256]{3,2,1,0:T(8,128)} %x_hbm.1), custom_call_target="tpu_custom_call" | custom-call | tf_op jit(solution)/shard_map/pallas_call | solution.py:632
  59.0 2.7 %shard_map.69 = (f32[116,256]{1,0:T(8,128)}, f32[2,58,16,256]{3,2,1,0:T(8,128)}) custom-call(f32[8,40,128]{2,1,0:T(8,128)} %get-tuple-element.7.land_hbm, f32[320,256]{1,0:T(8,128)} %get-tuple-element.8.give_hbm, f32[2,58,16,256]{3,2,1,0:T(8,128)} %get-tuple-element.9.state_hbm), custom_call_target="tpu_custom_call" | custom-call | tf_op jit(solution)/shard_map/pallas_call | solution.py:682
